TPU v7x, 32 devices: a whole 2x2x4 slice. The times are simulated.
32 devices in a mesh: seq: 4 (over z), fsdp: 8 (over y, x, core).
Axes of the slice: x: 2, y: 2, z: 4, core: 2. Of those that a mesh axis runs over, the one named last changes fastest.
Arguments:
- inputs: bfloat16 [8, 1024, 512], P('fsdp', 'seq'), may hold values from -6 to 6
- cotangent: bfloat16 [8, 1024, 512], P('fsdp', 'seq'), may hold values from -6 to 6
- lengths: int32 [8], P('fsdp'), may hold values from 256 to 1024, as said below
- square: float32 [4096, 512], P(('seq', 'fsdp')), may hold values from -0.25 to 0.25
- upward: float32 [4096, 512], P(('seq', 'fsdp')), may hold values from -0.25 to 0.25
- downward: float32 [4096, 512], P(('seq', 'fsdp')), may hold values from -0.125 to 0.125
- vectors: float32 [14, 512], P(None, ('seq', 'fsdp')), may hold values from 0.5 to 1.5
- kernel: float32 [31, 512], P(None, ('seq', 'fsdp')), may hold values from -1 to 1
- square_momentum: float32 [4096, 512], P(('seq', 'fsdp')), may hold values from -60 to 60
- square_variance: float32 [4096, 512], P(('seq', 'fsdp')), may hold values from 10 to 1000
- upward_momentum: float32 [4096, 512], P(('seq', 'fsdp')), may hold values from -60 to 60
- upward_variance: float32 [4096, 512], P(('seq', 'fsdp')), may hold values from 10 to 1000
- downward_momentum: float32 [4096, 512], P(('seq', 'fsdp')), may hold values from -60 to 60
- downward_variance: float32 [4096, 512], P(('seq', 'fsdp')), may hold values from 10 to 1000
- vectors_momentum: float32 [14, 512], P(None, ('seq', 'fsdp')), may hold values from -60 to 60
- vectors_variance: float32 [14, 512], P(None, ('seq', 'fsdp')), may hold values from 10 to 1000
- kernel_momentum: float32 [31, 512], P(None, ('seq', 'fsdp')), may hold values from -60 to 60
- kernel_variance: float32 [31, 512], P(None, ('seq', 'fsdp')), may hold values from 10 to 1000
Outputs:
- layer_output: bfloat16 [8, 1024, 512], P('fsdp', 'seq')
- input_grad: float32 [8, 1024, 512], P('fsdp', 'seq')
- square_grad: float32 [4096, 512], P(('seq', 'fsdp'))
- upward_grad: float32 [4096, 512], P(('seq', 'fsdp'))
- downward_grad: float32 [4096, 512], P(('seq', 'fsdp'))
- vectors_grad: float32 [14, 512], P(None, ('seq', 'fsdp'))
- kernel_grad: float32 [31, 512], P(None, ('seq', 'fsdp'))
- square_next: float32 [4096, 512], P(('seq', 'fsdp'))
- upward_next: float32 [4096, 512], P(('seq', 'fsdp'))
- downward_next: float32 [4096, 512], P(('seq', 'fsdp'))
- vectors_next: float32 [14, 512], P(None, ('seq', 'fsdp'))
- kernel_next: float32 [31, 512], P(None, ('seq', 'fsdp'))
- momentum_square: float32 [4096, 512], P(('seq', 'fsdp'))
- variance_square: float32 [4096, 512], P(('seq', 'fsdp'))
- momentum_upward: float32 [4096, 512], P(('seq', 'fsdp'))
- variance_upward: float32 [4096, 512], P(('seq', 'fsdp'))
- momentum_downward: float32 [4096, 512], P(('seq', 'fsdp'))
- variance_downward: float32 [4096, 512], P(('seq', 'fsdp'))
- momentum_vectors: float32 [14, 512], P(None, ('seq', 'fsdp'))
- variance_vectors: float32 [14, 512], P(None, ('seq', 'fsdp'))
- momentum_kernel: float32 [31, 512], P(None, ('seq', 'fsdp'))
- variance_kernel: float32 [31, 512], P(None, ('seq', 'fsdp'))
Inputs may be any that keep to these rules, and one draw needn't show every extreme that they name: `lengths`: every sequence has at least 256 valid frames; some sequence has exactly 256 and some exactly 1024.
All inputs are finite; a program needn't handle non-finite values.
Results may differ from a plain program's by a relative error of at most 0.017.
Values may be sent and summed in bfloat16 or wider, within the bound.
A program may use at most 192 MiB of HBM per device.

v0:
```python
import math

import jax
import jax.numpy as jnp
from jax import lax
from jax.experimental import pallas as pl
from jax.experimental.pallas import tpu as pltpu
from jax.sharding import PartitionSpec as P

D = 512
H = 8
FF = 2048
ADAM_STEP = 4

LN_EPS = 1e-05
BN_EPS = 1e-05
BETA_ONE = 0.9
BETA_TWO = 0.98
ADAM_EPS = 1e-08
LEARN_RATE = 0.005
DECAY_RATE = 0.01


def position_tables(seq_frames, model_width):
    fine = math.gcd(2 * seq_frames, 64)
    column = jnp.arange(model_width)
    frequency = jnp.exp(-math.log(10000.0) * 2.0 * (column // 2).astype(jnp.float32) / model_width)
    coarse_at = (seq_frames - 1 - fine * jnp.arange(2 * seq_frames // fine)).astype(jnp.float32)
    coarse_phase = coarse_at[:, None] * frequency[None, :]
    fine_phase = jnp.arange(fine).astype(jnp.float32)[:, None] * frequency[None, :]
    even = (column % 2 == 0)[None, :]
    sine, cosine = jnp.sin(coarse_phase), jnp.cos(coarse_phase)
    with_cosine = jnp.where(even, sine, cosine)
    with_sine = jnp.where(even, -cosine, sine)
    return jnp.stack([with_cosine, with_sine]), jnp.stack([jnp.cos(fine_phase), jnp.sin(fine_phase)])


def adam_step(weight, gradient, first_mom, second_mom, decay):
    first_new = BETA_ONE * first_mom + (1.0 - BETA_ONE) * gradient
    second_new = BETA_TWO * second_mom + (1.0 - BETA_TWO) * gradient * gradient
    fix_one = 1.0 - BETA_ONE**ADAM_STEP
    fix_two = 1.0 - BETA_TWO**ADAM_STEP
    update = first_new / fix_one / (jnp.sqrt(second_new / fix_two) + ADAM_EPS)
    return (weight - LEARN_RATE * (update + decay * weight), first_new, second_new)


MESH = pl.DeviceIdType.MESH
BF = jnp.bfloat16
F32 = jnp.float32
LANES = 128


class Grid:
    def __init__(self):
        self.nz = lax.axis_size("seq")
        self.nf = lax.axis_size("fsdp")
        plane = self.nf // 2
        side = math.isqrt(plane)
        self.z = lax.axis_index("seq")
        f = lax.axis_index("fsdp")
        self.core = f % 2
        if side * side == plane:
            self.na = self.nb = side
            self.step_a = 2 + self.core * (2 * side - 2)
            self.step_b = 2 * side - self.core * (2 * side - 2)
        else:
            self.na, self.nb = plane, 1
            self.step_a, self.step_b = 2, self.nf
        self.f = f
        self.a = (f // self.step_a) % self.na
        self.b = (f // self.step_b) % self.nb
        self.plane = plane
        self.chips = plane * self.nz

        self.half = self.nz // 2
        self.t = (self.z % self.half) * 2 + self.core
        self.column = f - self.core

    def time(self, q):
        return (self.z - self.z % self.half + q // 2, self.column + q % 2)

    def owner(self):
        return (self.t, self.column + self.z // self.half)

    def worker(self):
        return (self.core * self.half + self.z // 2, self.column + self.z % 2)

    def at_home(self):
        return jnp.logical_and(self.t == self.z, self.z // self.half == self.core)

    def chip(self, z, a, b):
        return z * self.plane + (a * self.step_a + b * self.step_b) // 2

    def device(self, z, a, b):
        return (z, a * self.step_a + b * self.step_b + self.core)

    def sibling(self):
        return (self.z, self.f + 1 - 2 * self.core)

    def up(self, axis):
        return self.device(self.z + (axis == "z"), self.a + (axis == "a"), self.b + (axis == "b"))

    def down(self, axis):
        return self.device(self.z - (axis == "z"), self.a - (axis == "a"), self.b - (axis == "b"))

    def line(self, axis):
        return {
            "c": (self.core, 2, lambda q: (self.z, self.f - self.core + q)),
            "a": (self.a, self.na, lambda q: self.device(self.z, q, self.b)),
            "b": (self.b, self.nb, lambda q: self.device(self.z, self.a, q)),
            "z": (self.z, self.nz, lambda q: self.device(q, self.a, self.b)),
        }[axis]

    def place(self, axis):
        return {"z": (self.z, self.nz), "a": (self.a, self.na), "b": (self.b, self.nb)}[axis]


def greet_mover(g, barrier, source):
    @pl.when(jnp.logical_not(g.at_home()))
    def _():
        pl.semaphore_signal(barrier, inc=1, device_id=source, device_id_type=MESH)

    return 1 - g.at_home().astype(jnp.int32)


def merge_moments(first_op, second_op):
    count = first_op[0:1] + second_op[0:1]
    share = second_op[0:1] / jnp.maximum(count, 1.0)
    gap = second_op[1:2] - first_op[1:2]
    mean = first_op[1:2] + gap * share
    squares = first_op[2:3] + second_op[2:3] + gap * gap * (first_op[0:1] * share)
    return jnp.concatenate([count, mean, squares, first_op[3:]], axis=0)


NT = (((1,), (1,)), ((), ()))
TN = (((0,), (0,)), ((), ()))
NN = (((1,), (0,)), ((), ()))


def dot(first_op, second_op, dims):
    return lax.dot_general(first_op, second_op, dims, preferred_element_type=F32)


def keep_head(value, h, head_size):
    lane = lax.broadcasted_iota(jnp.int32, value.shape, 1)
    return jnp.where(lane // head_size == h, value, jnp.zeros_like(value))


def attend_block(head_size, i, query_b, k_ref, v_ref, pos_ref, bias, len_ref, prob_ref):
    rows, cols = query_b.shape
    frames = k_ref.shape[0]
    width = rows + frames
    query = query_b.astype(F32)
    content = (query + bias[0:1, :]).astype(BF)
    positional = (query + bias[1:2, :]).astype(BF)
    window = pos_ref[pl.ds(pl.multiple_of(frames - rows - i * rows, rows), width), :]
    live = lax.broadcasted_iota(jnp.int32, (rows, frames), 1).astype(F32) < len_ref[0:1, 0:1]
    out = jnp.zeros((rows, cols), F32)
    for h in range(cols // head_size):
        direct = dot(keep_head(content, h, head_size), k_ref[...], NT)
        spread = dot(keep_head(positional, h, head_size), window, NT)
        shifted = pltpu.roll(spread, width - rows + 1, 1, stride=1, stride_axis=0)[:, :frames]
        score = jnp.where(live, (direct + shifted) * (1.0 / math.sqrt(head_size)), -1e30)
        top = jnp.max(score, axis=-1, keepdims=True)
        power = jnp.exp(score - top)
        prob_b = (power * (1.0 / jnp.sum(power, axis=-1, keepdims=True))).astype(BF)
        prob_ref[h] = prob_b
        out = out + keep_head(dot(prob_b, v_ref[...], NN), h, head_size)
    return out.astype(BF)


def attend_back_block(head_size, i, query_b, k_ref, v_ref, pos_ref, bias, prob_ref, grad_heads, gk_acc, gv_acc, gpos_acc, gbias):
    rows, cols = query_b.shape
    frames = k_ref.shape[0]
    width = rows + frames
    query = query_b.astype(F32)
    content = (query + bias[0:1, :]).astype(BF)
    positional = (query + bias[1:2, :]).astype(BF)
    down = lax.broadcasted_iota(jnp.int32, (rows, rows), 0)
    across = lax.broadcasted_iota(jnp.int32, (rows, rows), 1)
    turn = jnp.where(down + across == rows - 1, 1.0, 0.0).astype(BF)
    positional_turned = dot(turn, positional, NN).astype(BF)
    here = pl.ds(pl.multiple_of(frames - rows - i * rows, rows), width)
    window = pos_ref[here, :]
    grad_content = jnp.zeros((rows, cols), F32)
    grad_position = jnp.zeros((rows, cols), F32)
    for h in range(cols // head_size):
        grad_out = keep_head(grad_heads, h, head_size)
        prob_b = prob_ref[h]
        prob = prob_b.astype(F32)
        grad_prob = dot(grad_out, v_ref[...], NT)
        delta = jnp.sum(prob * grad_prob, axis=-1, keepdims=True)
        score_b = (prob * (grad_prob - delta) * (1.0 / math.sqrt(head_size))).astype(BF)
        grad_content = grad_content + keep_head(dot(score_b, k_ref[...], NN), h, head_size)
        gk_acc[...] += dot(keep_head(content, h, head_size), score_b, TN)
        gv_acc[...] += dot(grad_out, prob_b, TN)
        wide = jnp.concatenate([dot(turn, score_b, NN), jnp.zeros((rows, width - frames), F32)], axis=1)
        spread = pltpu.roll(wide, 0, 1, stride=1, stride_axis=0).astype(BF)
        grad_position = grad_position + keep_head(dot(spread, window, NN), h, head_size)
        gpos_acc[:, here] += dot(keep_head(positional_turned, h, head_size), spread, TN)
    high = grad_position.astype(BF)
    low = (grad_position - high.astype(F32)).astype(BF)
    grad_position = dot(turn, high, NN) + dot(turn, low, NN)
    gbias[0:1, :] += jnp.sum(grad_content, axis=0, keepdims=True)
    gbias[1:2, :] += jnp.sum(grad_position, axis=0, keepdims=True)
    return (grad_content + grad_position).astype(BF)

def normalize(value):
    mean = jnp.mean(value, axis=-1, keepdims=True)
    centred = value - mean
    spread = lax.rsqrt(jnp.mean(centred * centred, axis=-1, keepdims=True) + LN_EPS)
    return centred * spread, spread


def norm_forward(value, gains, k):
    unit, _ = normalize(value)
    return (unit * gains[2 * k : 2 * k + 1] + gains[2 * k + 1 : 2 * k + 2]).astype(BF)


def norm_backward(value, gains, k, upstream):
    unit, spread = normalize(value)
    inner = upstream * gains[2 * k : 2 * k + 1]
    along = jnp.mean(inner * unit, axis=-1, keepdims=True)
    grad = spread * (inner - jnp.mean(inner, axis=-1, keepdims=True) - unit * along)
    gain = jnp.sum(upstream * unit, axis=0, keepdims=True)
    return grad, gain, jnp.sum(upstream, axis=0, keepdims=True)


def sigmoid(value):
    return 1.0 / (1.0 + jnp.exp(-value))


def module_forward(normed, up_ref, down_ref, hidden_ref, active_ref):
    units, width = up_ref.shape
    step = min(512, units)

    def chunk(j, total):
        here = pl.ds(pl.multiple_of(j * step, step), step)
        hidden = dot(normed, up_ref[here, :], NT)
        active = (hidden * sigmoid(hidden)).astype(BF)
        hidden_ref[:, here] = hidden.astype(hidden_ref.dtype)
        active_ref[:, here] = active
        return total + dot(active, down_ref[here, :], NN)

    return lax.fori_loop(0, units // step, chunk, jnp.zeros((normed.shape[0], width), F32))


def module_backward(upstream_b, up_ref, down_ref, hidden_ref, grad_ref):
    units, width = up_ref.shape
    step = min(512, units)

    def chunk(j, total):
        here = pl.ds(pl.multiple_of(j * step, step), step)
        hidden = hidden_ref[:, here].astype(F32)
        sigma = sigmoid(hidden)
        slope = sigma * (1.0 + hidden * (1.0 - sigma))
        grad = (dot(upstream_b, down_ref[here, :], NT) * slope).astype(BF)
        grad_ref[:, here] = grad
        return total + dot(grad, up_ref[here, :], NN)

    return lax.fori_loop(0, units // step, chunk, jnp.zeros((upstream_b.shape[0], width), F32))


def greet_lines(g, axes, source=None):
    barrier = pltpu.get_barrier_semaphore()
    total = g.nz - 1
    for k in range(1, g.nz):
        pl.semaphore_signal(barrier, inc=1, device_id=g.time(lax.rem(g.t + k, g.nz)), device_id_type=MESH)
    if source is not None:
        total = total + greet_mover(g, barrier, source)
    for axis in axes:
        p, n, device = g.line(axis)
        for k in range(1, n):
            pl.semaphore_signal(barrier, inc=1, device_id=device(lax.rem(p + k, n)), device_id_type=MESH)
            total += 1
    pl.semaphore_wait(barrier, total)


def remote(src, dst, send, recv, device):
    return pltpu.make_async_remote_copy(
        src_ref=src, dst_ref=dst, send_sem=send, recv_sem=recv, device_id=device, device_id_type=MESH
    )


def arrived(ref, sem):
    pltpu.make_async_copy(ref, ref, sem).wait()


def meet_levels(g, value, merge, buf, send_sem, recv_sem):
    sends = []
    for level, axis in enumerate("cabz"):
        p, n, device = g.line(axis)
        if n == 1:
            continue
        buf[level, p] = value
        for k in range(1, n):
            copy = remote(buf.at[level, p], buf.at[level, p], send_sem.at[level, k], recv_sem.at[level, p], device(lax.rem(p + k, n)))
            copy.start()
            sends.append(copy)
        for k in range(1, n):
            q = lax.rem(p + k, n)
            arrived(buf.at[level, q], recv_sem.at[level, q])
        value = buf[level, 0]
        for q in range(1, n):
            value = merge(value, buf[level, q])
    return value, sends


HALO = 16


def swap_edges(g, body, low, high, send_sem, recv_sem, pad):
    rows = body.shape[0]
    p, n = g.t, g.nz
    up = remote(body.at[pl.ds(rows - HALO, HALO)], low, send_sem.at[0], recv_sem.at[0], g.time(p + 1))
    down = remote(body.at[pl.ds(0, HALO)], high, send_sem.at[1], recv_sem.at[1], g.time(p - 1))
    pl.when(p < n - 1)(lambda: up.start())
    pl.when(p > 0)(lambda: down.start())
    pad[pl.ds(HALO, rows), :] = body[...].astype(F32)

    def fill(at, ref, sem, there):
        @pl.when(there)
        def _():
            arrived(ref, sem)
            pad[pl.ds(at, HALO), :] = ref[...].astype(F32)

        @pl.when(jnp.logical_not(there))
        def _():
            pad[pl.ds(at, HALO), :] = jnp.zeros((HALO, pad.shape[1]), F32)

    fill(0, low, recv_sem.at[0], p > 0)
    fill(HALO + rows, high, recv_sem.at[1], p < n - 1)

    def finish():
        pl.when(p < n - 1)(lambda: up.wait_send())
        pl.when(p > 0)(lambda: down.wait_send())

    return finish


def middle_kernel(taps, len_ref, att_ref, x1_ref, cot_ref, gains_ref, ud_hbm, sq_hbm,
                  y_ref, g2_ref, go_ref, o_ref, e2_ref, a3_ref, gpair_ref, e3_ref, sw_ref, a4_ref, s4_ref, gh4_ref, e4_ref,
                  small_ref, gtaps_ref,
                  up, down, wsq, o_buf, go_buf, glu_b, gc_b, low1, high1, low2, high2, pad_glu, pad_gc, h4, c_ref, y_buf, y_sem,
                  buf1, buf2, load_sem, a_send, a_recv, b_send, b_recv, h_send, h_recv, m_send, m_recv):
    g = Grid()
    z, nz = g.t, g.nz
    rows, width = x1_ref.shape
    cols = width // nz
    units = up.shape[0]
    rim = (taps - 1) // 2
    loads = [
        pltpu.make_async_copy(sq_hbm.at[pl.ds(4 * width, 4 * width)], wsq, load_sem.at[0]),
        pltpu.make_async_copy(ud_hbm.at[0, pl.ds(units, units)], up, load_sem.at[1]),
        pltpu.make_async_copy(ud_hbm.at[1, pl.ds(units, units)], down, load_sem.at[2]),
    ]
    for load in loads:
        load.start()
    greet_lines(g, "cabz", g.worker())
    sends = []
    for k in range(1, nz):
        q = lax.rem(z + k, nz)
        copy = remote(att_ref.at[pl.ds(q * rows, rows)], o_buf.at[z], a_send.at[k], a_recv.at[z], g.time(q))
        copy.start()
        sends.append(copy)
    o_buf[z] = att_ref[pl.ds(pl.multiple_of(z * rows, rows), rows), :]
    gains = gains_ref[...]
    frame = z * rows + lax.broadcasted_iota(jnp.int32, (rows, 1), 0)
    live = jnp.where(frame.astype(F32) < len_ref[0:1, 0:1], 1.0, 0.0)
    loads[0].wait()
    weight = lambda k: wsq[pl.ds((k - 4) * width, width), :]
    for k in range(1, nz):
        q = lax.rem(z + k, nz)
        arrived(o_buf.at[q], a_recv.at[q])
    out = jnp.concatenate([o_buf[q] for q in range(nz)], axis=1)
    o_ref[...] = out
    resid2 = x1_ref[...] + dot(out, weight(4), NT)
    normed3 = norm_forward(resid2, gains, 2)
    a3_ref[...] = normed3
    value = dot(normed3, weight(5), NT)
    gate = sigmoid(dot(normed3, weight(6), NT))
    glu_b[...] = (value * gate * live).astype(BF)
    done1 = swap_edges(g, glu_b, low1, high1, h_send.at[0], h_recv.at[0], pad_glu)
    for at in range(0, width, LANES):
        lanes = pl.ds(at, LANES)
        total = jnp.zeros((rows, LANES), F32)
        for m in range(taps):
            total = total + gains_ref[14 + m : 15 + m, lanes] * pad_glu[pl.ds(HALO - rim + m, rows), lanes]
        c_ref[:, lanes] = total
    conv = c_ref[...]
    count = jnp.sum(live, axis=0, keepdims=True)
    mean = jnp.sum(live * conv, axis=0, keepdims=True) / jnp.maximum(count, 1.0)
    squares = jnp.sum(live * (conv - mean) * (conv - mean), axis=0, keepdims=True)
    moments = jnp.concatenate([jnp.broadcast_to(count, mean.shape), mean, squares, jnp.zeros((5, width), F32)], axis=0)
    moments, more = meet_levels(g, moments, merge_moments, buf1, m_send.at[0], m_recv.at[0])
    sends += more
    total_frames = moments[0:1]
    inv_std = lax.rsqrt(moments[2:3] / total_frames + BN_EPS)
    centre = moments[1:2]
    centred = c_ref[...] - centre
    zed = centred * inv_std
    bn_val = gains[12:13] * zed + gains[13:14]
    swish = (bn_val * sigmoid(bn_val)).astype(BF)
    sw_ref[...] = swish
    resid3 = resid2 + dot(swish, weight(7), NT)
    normed4 = norm_forward(resid3, gains, 3)
    a4_ref[...] = normed4
    loads[1].wait()
    loads[2].wait()
    resid4 = resid3 + 0.5 * module_forward(normed4, up, down, h4, s4_ref)
    y_buf[...] = norm_forward(resid4, gains, 4)
    away = jnp.logical_not(g.at_home())
    home = remote(y_buf, y_ref, y_sem.at[0], y_sem.at[1], g.owner())
    pl.when(away)(lambda: home.start())

    @pl.when(g.at_home())
    def _():
        y_ref[...] = y_buf[...]

    grad4, gain4, shift4 = norm_backward(resid4, gains, 4, cot_ref[...].astype(F32))
    half4 = (0.5 * grad4).astype(BF)
    e4_ref[...] = half4
    grad_norm, gain3, shift3 = norm_backward(resid3, gains, 3, module_backward(half4, up, down, h4, gh4_ref))
    grad3 = grad4 + grad_norm
    e3 = grad3.astype(BF)
    e3_ref[...] = e3
    sigma = sigmoid(bn_val)
    grad_bn = dot(e3, weight(7), NN) * (sigma * (1.0 + bn_val * (1.0 - sigma)))
    gamma = jnp.sum(grad_bn * zed, axis=0, keepdims=True)
    beta = jnp.sum(grad_bn, axis=0, keepdims=True)
    grad_zed = grad_bn * gains[12:13]
    sum_one = jnp.sum(grad_zed, axis=0, keepdims=True)
    sum_two = jnp.sum(grad_zed * centred, axis=0, keepdims=True)
    sums = jnp.concatenate([sum_one, sum_two, jnp.zeros((6, width), F32)], axis=0)
    sums, more = meet_levels(g, sums, lambda x, y: x + y, buf2, m_send.at[1], m_recv.at[1])
    sends += more
    offset = inv_std * sums[0:1] + inv_std * inv_std * inv_std * sums[1:2] * centred
    gc_b[...] = (inv_std * grad_zed - live / total_frames * offset).astype(BF)
    done2 = swap_edges(g, gc_b, low2, high2, h_send.at[1], h_recv.at[1], pad_gc)
    for at in range(0, width, LANES):
        lanes = pl.ds(at, LANES)
        total = jnp.zeros((rows, LANES), F32)
        upstream = pad_gc[pl.ds(HALO, rows), lanes]
        for m in range(taps):
            total = total + gains_ref[14 + m : 15 + m, lanes] * pad_gc[pl.ds(HALO + rim - m, rows), lanes]
            gtaps_ref[m : m + 1, lanes] = jnp.sum(
                upstream * pad_glu[pl.ds(HALO - rim + m, rows), lanes], axis=0, keepdims=True
            )
        c_ref[:, lanes] = total
    grad_glu = c_ref[...] * live
    gv5 = (grad_glu * gate).astype(BF)
    gv6 = (grad_glu * value * gate * (1.0 - gate)).astype(BF)
    gpair_ref[0] = gv5
    gpair_ref[1] = gv6
    grad_norm, gain2, shift2 = norm_backward(
        resid2, gains, 2, dot(gv5, weight(5), NN) + dot(gv6, weight(6), NN)
    )
    grad2 = grad3 + grad_norm
    g2_ref[...] = grad2
    e2 = grad2.astype(BF)
    e2_ref[...] = e2
    grad_out = dot(e2, weight(4), NN).astype(BF)
    for q in range(nz):
        go_buf[q] = grad_out[:, q * cols : (q + 1) * cols]
    for k in range(1, nz):
        q = lax.rem(z + k, nz)
        copy = remote(go_buf.at[q], go_ref.at[pl.ds(z * rows, rows)], b_send.at[k], b_recv.at[z], g.time(q))
        copy.start()
        sends.append(copy)
    go_ref[pl.ds(pl.multiple_of(z * rows, rows), rows), :] = go_buf[z]
    small_ref[...] = jnp.concatenate([gain2, shift2, gain3, shift3, gain4, shift4, gamma, beta], axis=0)
    for k in range(1, nz):
        q = lax.rem(z + k, nz)
        arrived(go_ref.at[pl.ds(q * rows, rows)], b_recv.at[q])
    pl.when(away)(lambda: home.wait())
    done1()
    done2()
    for copy in sends:
        copy.wait_send()


def middle(length, attended, resid1, cotangent, gains, taps, ud_full, sq_full):
    rows, width = resid1.shape
    nz, nf = lax.axis_size("seq"), lax.axis_size("fsdp")
    frames, cols = rows * nz, width // nz
    units = ud_full.shape[1] // 2
    most = max(nz, nf // 2)
    vmem = pl.BlockSpec(memory_space=pltpu.VMEM)
    hbm = pl.BlockSpec(memory_space=pl.ANY)
    shape = jax.ShapeDtypeStruct
    dma = pltpu.SemaphoreType.DMA
    row = shape((rows, width), BF)
    return pl.pallas_call(
        lambda *refs: middle_kernel(taps, *refs),
        name="middle",
        out_shape=(
            row,
            shape((rows, width), F32),
            shape((frames, cols), BF),
            row,
            row,
            row,
            shape((2, rows, width), BF),
            row,
            row,
            row,
            shape((rows, units), BF),
            shape((rows, units), BF),
            row,
            shape((8, width), F32),
            shape((taps, width), F32),
        ),
        in_specs=[vmem] * 5 + [hbm] * 2,
        out_specs=[vmem] * 15,
        scratch_shapes=[
            pltpu.VMEM((units, width), BF),
            pltpu.VMEM((units, width), BF),
            pltpu.VMEM((4 * width, width), BF),
            pltpu.VMEM((nz, rows, cols), BF),
            pltpu.VMEM((nz, rows, cols), BF),
            pltpu.VMEM((rows, width), BF),
            pltpu.VMEM((rows, width), BF),
        ]
        + [pltpu.VMEM((HALO, width), BF)] * 4
        + [
            pltpu.VMEM((rows + 2 * HALO, width), F32),
            pltpu.VMEM((rows + 2 * HALO, width), F32),
            pltpu.VMEM((rows, units), F32),
            pltpu.VMEM((rows, width), F32),
            pltpu.VMEM((rows, width), BF),
            dma((2,)),
            pltpu.VMEM((4, most, 8, width), F32),
            pltpu.VMEM((4, most, 8, width), F32),
            dma((3,)),
            dma((nz,)),
            dma((nz,)),
            dma((nz,)),
            dma((nz,)),
            dma((2, 2)),
            dma((2, 2)),
            dma((2, 4, most)),
            dma((2, 4, most)),
        ],
        compiler_params=pltpu.CompilerParams(
            collective_id=6, has_side_effects=True, vmem_limit_bytes=56 * 1024 * 1024
        ),
    )(length, attended, resid1, cotangent, gains, ud_full, sq_full)


class Meeting:
    def __init__(self, g, buf, send_sem, recv_sem):
        self.g, self.buf, self.send_sem, self.recv_sem = g, buf, send_sem, recv_sem
        self.sends = []

    def start(self, level, value):
        axis = "cabz"[level]
        p, n, device = self.g.line(axis)
        self.buf[level, p] = value
        for k in range(1, n):
            here = self.buf.at[level, p]
            copy = remote(here, here, self.send_sem.at[level, k], self.recv_sem.at[level, p], device(lax.rem(p + k, n)))
            copy.start()
            self.sends.append(copy)

    def total(self, level):
        p, n, _ = self.g.line("cabz"[level])
        for k in range(1, n):
            q = lax.rem(p + k, n)
            arrived(self.buf.at[level, q], self.recv_sem.at[level, q])
        value = self.buf[level, 0]
        for q in range(1, n):
            value = value + self.buf[level, q]
        return value


class Reduction:
    def __init__(self, g, gud, gsq, sib_ud, sib_sq, sib_sem, rb, ra, rz, sems):
        self.g, self.gud, self.gsq, self.sib_ud, self.sib_sq = g, gud, gsq, sib_ud, sib_sq
        self.sib_send, self.sib_recv = sib_sem
        self.bufs = {"b": rb, "a": ra, "z": rz}
        self.sems = sems
        self.sq_rows = gsq.shape[2]
        self.pair = 2 * self.sq_rows
        self.height = g.plane * self.pair

    def rows(self, t, part):
        return pl.ds(pl.multiple_of(t * self.pair + (part - 1) * self.sq_rows, self.sq_rows), self.sq_rows)

    def own(self, t, part):
        c = self.g.core
        return self.gsq.at[t, c] if part == 0 else self.gud.at[c, self.rows(t, part)]

    def sibling_copy(self, z, kind):
        g = self.g
        d = 1 - g.core
        if kind == 0:
            chips = pl.ds(z * g.plane, g.plane)
            src, dst = self.gsq.at[chips, d], self.sib_sq.at[chips]
        else:
            tall = pl.ds(z * self.height, self.height)
            src, dst = self.gud.at[d, tall], self.sib_ud.at[tall]
        return remote(src, dst, self.sib_send.at[kind, z], self.sib_recv.at[kind, z], g.sibling())

    def to_sibling(self, planes, kind):
        for z in planes:
            self.sibling_copy(z, kind).start()

    def from_sibling(self, planes, kind):
        for z in planes:
            self.sibling_copy(z, kind).wait_recv()

    def add_sibling(self, t, part):
        ref = self.own(t, part)
        ref[...] = ref[...] + (self.sib_sq[t] if part == 0 else self.sib_ud[self.rows(t, part), :])

    def landing(self, axis, slot, part):
        return self.bufs[axis].at[slot, pl.ds(part * self.sq_rows, self.sq_rows)]

    def slot(self, axis, upward, z, a, b, there):
        g = self.g
        p, n = g.place(axis)
        q = {"z": z, "a": a, "b": b}[axis]
        if there:
            p = p + 1 if upward else p - 1
        if upward:
            q = q + 1 - n * (p == n - 1)
        return {"b": (q * g.na + a) * g.nz + z, "a": q * g.nz + z, "z": q}[axis]

    def hop(self, axis, upward, z, a, b, part):
        g = self.g
        slot = self.slot(axis, upward, z, a, b, True)
        sends, recvs = self.sems[axis]
        device = g.up(axis) if upward else g.down(axis)
        src, dst = self.own(g.chip(z, a, b), part), self.landing(axis, slot, part)
        return remote(src, dst, sends.at[1 if upward else 0, part, slot], recvs.at[part, slot], device)

    def take(self, axis, upward, z, a, b, part):
        slot = self.slot(axis, upward, z, a, b, False)
        src, dst = self.landing(axis, slot, part), self.own(self.g.chip(z, a, b), part)
        arrived(src, self.sems[axis][1].at[part, slot])
        dst[...] = dst[...] + src[...]

    def settle(self, axis, z, a, b, part):
        p, n = self.g.place(axis)
        if n > 1:
            pl.when(p > 0)(lambda: self.take(axis, True, z, a, b, part))
            pl.when(p < n - 1)(lambda: self.take(axis, False, z, a, b, part))

    def ready(self, axis, z, a, b, part):
        if axis == "b":
            self.add_sibling(self.g.chip(z, a, b), part)
        else:
            before = {"a": "b", "z": "a"}[axis]
            self.ready(before, z, a, b, part)
            self.settle(before, z, a, b, part)

    def pass_on(self, axis, upward, z, a, b, part, finish):
        p, n = self.g.place(axis)
        if finish:
            self.hop(axis, upward, z, a, b, part).wait_send()
            return
        self.ready(axis, z, a, b, part)
        behind = p > 0 if upward else p < n - 1
        pl.when(behind)(lambda: self.take(axis, upward, z, a, b, part))
        self.hop(axis, upward, z, a, b, part).start()

    def along(self, axis, planes, part, finish=False):
        g = self.g
        p, n = g.place(axis)
        if axis == "z":
            for q in planes:
                pl.when(p < q)(lambda: self.pass_on("z", True, q, g.a, g.b, part, finish))
                pl.when(p > q)(lambda: self.pass_on("z", False, q, g.a, g.b, part, finish))
            return
        step = planes[1] - planes[0] if len(planes) > 1 else 1
        count = len(planes)
        for k in range(n - 1, 0, -1):
            for upward in (True, False):
                q = p + k if upward else p - k

                def act():
                    def body(i, _):
                        plane = planes[0] + step * lax.rem(i, count)
                        if axis == "b":
                            a = lax.rem(g.a + 1 + i // count, g.na)
                            self.pass_on("b", upward, plane, a, q, part, finish)
                        else:
                            self.pass_on("a", upward, plane, q, g.b, part, finish)
                        return 0

                    lax.fori_loop(0, (g.na if axis == "b" else 1) * count, body, 0)

                pl.when(p + k < n if upward else p >= k)(act)

    def last(self, part):
        g = self.g
        self.ready("z", g.z, g.a, g.b, part)
        self.settle("z", g.z, g.a, g.b, part)


def back_kernel(head_size, qkv_ref, pos_ref, go_ref, coarse_ref, fine_ref, gains_ref,
                x_ref, x1_ref, g2_ref, a1_ref, h1_ref, s1_ref, a2_ref,
                a4_ref, s4_ref, gh4_ref, e4_ref, o_ref, e2_ref, a3_ref, gpair_ref, e3_ref, sw_ref, some_ref, gtaps_ref,
                prob_hbm, ud_hbm, sq_hbm,
                gx_ref, ud_out, sq_out, small_out,
                prob_buf, gk_acc, gv_acc, gpos_acc, gbias, grads, prob_sem, wqkv, heads, gqkv, gh1, small, gud, gsq, sib_ud, sib_sq, rb, ra, rz, sbuf, fin_send_buf, fin, gx_buf, gx_in, gx_sem,
                load_sem, h_send, h_recv, sib_send, sib_recv, b_send, b_recv, a_send, a_recv, z_send, z_recv, s_send, s_recv,
                fin_send, fin_recv):
    g = Grid()
    z, nz, c = g.t, g.nz, g.core
    rows, width = x_ref.shape
    cols = width // nz
    units = h1_ref.shape[1]
    frames = qkv_ref.shape[1]
    up, down = gud.at[0, pl.ds(0, units)], gud.at[1, pl.ds(0, units)]
    loads = [
        pltpu.make_async_copy(sq_hbm.at[pl.ds(0, 3 * width)], wqkv, load_sem.at[0]),
        pltpu.make_async_copy(ud_hbm.at[0, pl.ds(0, units)], up, load_sem.at[1]),
        pltpu.make_async_copy(ud_hbm.at[1, pl.ds(0, units)], down, load_sem.at[2]),
    ]

    def probabilities(i):
        return pltpu.make_async_copy(prob_hbm.at[:, pl.ds(i * rows, rows)], prob_buf.at[i % 2], prob_sem.at[i % 2])

    probabilities(0).start()
    for load in loads:
        load.start()
    greet_lines(g, "cabz", g.worker())
    sends = []
    red = Reduction(
        g, gud, gsq, sib_ud, sib_sq, (sib_send, sib_recv), rb, ra, rz,
        {"b": (b_send, b_recv), "a": (a_send, a_recv), "z": (z_send, z_recv)},
    )
    total_rows = gud.shape[1]
    sq_rows = gsq.shape[2]
    high = list(range(nz - 1, nz // 2 - 1, -1))
    low = list(range(0, nz // 2))
    part = 256

    def matrix_terms(color, left_ref, right, first_row, count):
        def body(i, _):
            here = pl.ds(pl.multiple_of(i * part, part), part)
            there = pl.ds(pl.multiple_of(first_row + i * part, part), part)
            gud[color, there, :] = dot(left_ref[:, here], right, TN).astype(BF)
            return 0

        lax.fori_loop(0, count // part, body, 0)

    per = width // sq_rows // 2

    def square_terms(block, left, right):
        sums = dot(left, right, TN).astype(BF).reshape(per, 2, sq_rows, width)
        gsq[pl.ds(block * per, per)] = sums

    square_terms(7, e3_ref[...], sw_ref[...])
    square_terms(6, gpair_ref[1], a3_ref[...])
    square_terms(5, gpair_ref[0], a3_ref[...])
    square_terms(4, e2_ref[...], o_ref[...])
    red.to_sibling(high, 0)
    matrix_terms(0, gh4_ref, a4_ref[...], units, units)
    matrix_terms(1, s4_ref, e4_ref[...], units, units)
    red.to_sibling(high, 1)
    gk_acc[...] = jnp.zeros_like(gk_acc)
    gv_acc[...] = jnp.zeros_like(gv_acc)
    gpos_acc[...] = jnp.zeros_like(gpos_acc)
    gbias[...] = jnp.zeros_like(gbias)
    to_time = lambda j, q, k: remote(grads.at[j, q], heads.at[j, z], h_send.at[j, k], h_recv.at[j, z], g.time(q))
    bias = gains_ref[10:12, pl.ds(pl.multiple_of(z * cols, cols), cols)]

    def attend(i, _):
        pl.when(i + 1 < nz)(lambda: probabilities(i + 1).start())
        probabilities(i).wait()
        here = pl.ds(pl.multiple_of(i * rows, rows), rows)
        grads[0, i] = attend_back_block(
            head_size, i, qkv_ref[0, here, :], qkv_ref.at[1], qkv_ref.at[2], pos_ref, bias, prob_buf.at[i % 2],
            go_ref[here, :], gk_acc, gv_acc, gpos_acc, gbias,
        )

        @pl.when(i == 0)
        def _():
            red.from_sibling(high, 0)
            red.along("b", high, 0)

        @pl.when(i == 1)
        def _():
            red.from_sibling(high, 1)
            red.along("b", high, 1)
            red.along("b", high, 2)

        return 0

    lax.fori_loop(0, nz, attend, 0)
    grads_k = gk_acc[...].T.astype(BF)
    grads_v = gv_acc[...].T.astype(BF)
    for q in range(nz):
        grads[1, q] = grads_k[q * rows : (q + 1) * rows]
        grads[2, q] = grads_v[q * rows : (q + 1) * rows]
    for k in range(1, nz):
        q = lax.rem(z + k, nz)
        for j in range(3):
            copy = to_time(j, q, k)
            copy.start()
            sends.append(copy)
    for j in range(3):
        heads[j, z] = grads[j, z]
    red.along("a", high, 0)
    fine = fine_ref.shape[1]

    def position(i, total):
        table = coarse_ref[0, pl.ds(2 * i, 1), :] * fine_ref[0] + coarse_ref[1, pl.ds(2 * i, 1), :] * fine_ref[1]
        after = coarse_ref[0, pl.ds(2 * i + 1, 1), :] * fine_ref[0] + coarse_ref[1, pl.ds(2 * i + 1, 1), :] * fine_ref[1]
        both = jnp.concatenate([table, after], axis=0).astype(BF)
        return total + dot(gpos_acc[:, pl.ds(pl.multiple_of(i * 2 * fine, 2 * fine), 2 * fine)].astype(BF), both, NN)

    gpos = lax.fori_loop(0, coarse_ref.shape[1] // 2, position, jnp.zeros((cols, width), F32)).astype(BF)
    gsq[pl.ds(3 * per, per)] = jnp.zeros((per, 2, sq_rows, width), BF)
    pieces = cols // sq_rows
    for i in range(pieces):
        piece = z * pieces + i
        gsq[3 * per + piece // 2, piece % 2] = gpos[i * sq_rows : (i + 1) * sq_rows]
    gains = gains_ref[...]
    loads[0].wait()
    grad_norm = jnp.zeros((rows, width), F32)
    for j in range(3):
        for k in range(1, nz):
            q = lax.rem(z + k, nz)
            arrived(heads.at[j, q], h_recv.at[j, q])
        full = jnp.concatenate([heads[j, q] for q in range(nz)], axis=1)
        gqkv[j] = full
        grad_norm = grad_norm + dot(full, wqkv[pl.ds(j * width, width), :], NN)
    for j in range(3):
        square_terms(j, gqkv[j], a2_ref[...])
    red.to_sibling(low, 0)
    resid1 = x1_ref[...]
    grad_add, gain1, shift1 = norm_backward(resid1, gains, 1, grad_norm)
    grad1 = g2_ref[...] + grad_add
    half1 = (0.5 * grad1).astype(BF)
    loads[1].wait()
    loads[2].wait()
    red.along("a", high, 1)
    grad_norm = module_backward(half1, up, down, h1_ref, gh1)
    red.from_sibling(low, 0)
    red.along("b", low, 0)
    matrix_terms(0, gh1, a1_ref[...], 0, units)
    matrix_terms(1, s1_ref, half1, 0, units)
    red.to_sibling(low, 1)
    red.along("a", high, 2)
    grad_add, gain0, shift0 = norm_backward(x_ref[...].astype(F32), gains, 0, grad_norm)
    away = jnp.logical_not(g.at_home())
    gx_buf[...] = (grad1 + grad_add).astype(BF)
    home = remote(gx_buf, gx_in, gx_sem.at[0], gx_sem.at[1], g.owner())
    pl.when(away)(lambda: home.start())
    small[...] = jnp.zeros_like(small)
    small[0:1, :] = gain0
    small[1:2, :] = shift0
    small[2:3, :] = gain1
    small[3:4, :] = shift1
    small[4:10, :] = some_ref[0:6, :]
    small[10:12, pl.ds(pl.multiple_of(z * cols, cols), cols)] = gbias[...]
    small[12:14, :] = some_ref[6:8, :]
    small[14 : 14 + gtaps_ref.shape[0], :] = gtaps_ref[...]
    meeting = Meeting(g, sbuf, s_send, s_recv)
    meeting.start(0, small[...])
    red.from_sibling(low, 1)
    red.along("b", low, 1)
    red.along("b", low, 2)
    red.along("a", low, 0)
    meeting.start(1, meeting.total(0))
    red.along("z", high, 0)
    red.along("z", high, 1)
    red.along("a", low, 1)
    red.along("z", low, 0)
    meeting.start(2, meeting.total(1))
    red.along("z", high, 2)
    red.along("a", low, 2)
    red.along("z", low, 1)
    meeting.start(3, meeting.total(2))
    red.along("z", low, 2)
    for part in range(3):
        red.last(part)
    me = g.chip(g.z, g.a, g.b)
    d = 1 - c
    half = ud_out.shape[1]
    at = lambda k: pl.ds(pl.multiple_of(me * 2 * half + k * half, half), half)
    fin_send_buf[...] = gud[c, at(d), :]
    swap = remote(fin_send_buf, fin, fin_send, fin_recv, g.sibling())
    swap.start()
    ud_out[c] = gud[c, at(c), :].astype(F32)
    sq_out[...] = gsq[me, c].astype(F32)
    small_out[...] = meeting.total(3)
    for planes in (high, low):
        for part in range(3):
            for axis in "baz":
                red.along(axis, planes, part, True)
        for kind in range(2):
            for q in planes:
                red.sibling_copy(q, kind).wait_send()
    for copy in sends + meeting.sends:
        copy.wait_send()

    @pl.when(away)
    def _():
        home.wait()
        gx_ref[...] = gx_in[...].astype(F32)

    @pl.when(g.at_home())
    def _():
        gx_ref[...] = gx_buf[...].astype(F32)

    swap.wait()
    ud_out[d] = fin[...].astype(F32)


def back(qkv, pos, grad_out, prob, head_size, coarse, fine, gains, signal, resid1, grad2, first, second, squares, some, gtaps, ud_full, sq_full):
    rows, width = signal.shape
    nz, nf = lax.axis_size("seq"), lax.axis_size("fsdp")
    chips = nz * nf // 2
    plane = nf // 2
    side = math.isqrt(plane)
    na, nb = (side, side) if side * side == plane else (plane, 1)
    cols = width // nz
    units = ud_full.shape[1] // 2
    own = ud_full.shape[1] // (2 * chips)
    block = 3 * own
    most = max(nz, na, nb, 2)
    tall = -(-(14 + gtaps.shape[0]) // 8) * 8
    vmem = pl.BlockSpec(memory_space=pltpu.VMEM)
    hbm = pl.BlockSpec(memory_space=pl.ANY)
    shape = jax.ShapeDtypeStruct
    dma = pltpu.SemaphoreType.DMA
    frames = rows * nz
    heads = cols // head_size
    operands = (qkv, pos, grad_out, coarse, fine, gains, signal, resid1, grad2, *first, *second, *squares, some, gtaps)
    places = lambda n: n + 1 if n > 2 else 1
    slots = {"b": places(nb) * na * nz, "a": places(na) * nz, "z": places(nz)}
    return pl.pallas_call(
        lambda *refs: back_kernel(head_size, *refs),
        name="back",
        out_shape=(
            shape((rows, width), F32),
            shape((2, own, width), F32),
            shape((own, width), F32),
            shape((tall, width), F32),
        ),
        in_specs=[vmem] * len(operands) + [hbm] * 3,
        out_specs=[vmem] * 4,
        scratch_shapes=[
            pltpu.VMEM((2, heads, rows, frames), BF),
            pltpu.VMEM((cols, frames), F32),
            pltpu.VMEM((cols, frames), F32),
            pltpu.VMEM((cols, 2 * frames), F32),
            pltpu.VMEM((2, cols), F32),
            pltpu.VMEM((3, nz, rows, cols), BF),
            dma((2,)),
            pltpu.VMEM((3 * width, width), BF),
            pltpu.VMEM((3, nz, rows, cols), BF),
            pltpu.VMEM((3, rows, width), BF),
            pltpu.VMEM((rows, units), BF),
            pltpu.VMEM((tall, width), F32),
            pltpu.VMEM((2, 2 * units, width), BF),
            pltpu.VMEM((chips, 2, own, width), BF),
            pltpu.VMEM((2 * units, width), BF),
            pltpu.VMEM((chips, own, width), BF),
            pltpu.VMEM((slots["b"], block, width), BF),
            pltpu.VMEM((slots["a"], block, width), BF),
            pltpu.VMEM((slots["z"], block, width), BF),
            pltpu.VMEM((4, most, tall, width), F32),
            pltpu.VMEM((own, width), BF),
            pltpu.VMEM((own, width), BF),
            pltpu.VMEM((rows, width), BF),
            pltpu.VMEM((rows, width), BF),
            dma((2,)),
            dma((3,)),
            dma((3, nz)),
            dma((3, nz)),
            dma((2, nz)),
            dma((2, nz)),
            dma((2, 3, slots["b"])),
            dma((3, slots["b"])),
            dma((2, 3, slots["a"])),
            dma((3, slots["a"])),
            dma((2, 3, slots["z"])),
            dma((3, slots["z"])),
            dma((4, most)),
            dma((4, most)),
            dma,
            dma,
        ],
        compiler_params=pltpu.CompilerParams(
            collective_id=7, has_side_effects=True, vmem_limit_bytes=61000 * 1024
        ),
    )(*operands, prob, ud_full, sq_full)


def when(*conditions):
    holds = 1
    for condition in conditions:
        holds = holds * jnp.asarray(condition).astype(jnp.int32)
    return pl.when(holds == 1) if conditions else lambda act: act()


class Gather:
    WAYS = {"z+": 0, "z-": 1, "a+": 2, "a-": 3, "b+": 4, "b-": 5, "s": 6}
    PARTS = (0, 1, 2)
    SPREAD = ("a+", "a-", "b+", "b-", "s")

    def __init__(self, g, ud, sq, recv_sem, sib_recv, send_sem):
        self.g, self.ud, self.sq = g, ud, sq
        self.recv_sem, self.sib_recv, self.send_sem = recv_sem, sib_recv, send_sem
        self.rows = sq.shape[2]
        half = g.nz // 2
        if half == 2:
            first = jnp.minimum(g.z, 1)
            second = jnp.maximum(g.z, 2)
            self.low, self.high = [first, 1 - first], [second, 5 - second]
        else:
            self.low, self.high = list(range(half)), list(range(half, g.nz))
        self.below = g.z < half

    def piece(self, part, t, color):
        if part == 0:
            return self.sq.at[t, color]
        return self.ud.at[color, pl.ds(t * 2 * self.rows + (part - 1) * self.rows, self.rows)]

    def onward(self, part, t, ways, finish, *only):
        g = self.g
        ref = self.piece(part, t, g.core)
        for way in ways:
            p, n = (0, 2) if way == "s" else g.place(way[0])

            def act():
                if way == "s":
                    target, arrive = g.sibling(), self.sib_recv
                else:
                    target, arrive = g.up(way[0]) if way[1] == "+" else g.down(way[0]), self.recv_sem
                copy = remote(ref, ref, self.send_sem.at[self.WAYS[way], part, t], arrive.at[part, t], target)
                copy.wait_send() if finish else copy.start()

            if way == "s":
                when(*only)(act)
            elif n > 1:
                when(*only, p < n - 1 if way[1] == "+" else p > 0)(act)

    def wait(self, part, t, finish):
        if not finish:
            arrived(self.piece(part, t, self.g.core), self.recv_sem.at[part, t])

    def column(self, q, spread, finish, *only):
        g = self.g
        t = g.chip(q, g.a, g.b)
        for part in self.PARTS:
            when(*only, q != g.z)(lambda: self.wait(part, t, finish))
            self.onward(part, t, ("z+",), finish, *only, q <= g.z)
            self.onward(part, t, ("z-",), finish, *only, q >= g.z)
            if spread:
                self.onward(part, t, self.SPREAD, finish, *only)

    def spread(self, q, finish, *only):
        g = self.g
        for part in self.PARTS:
            self.onward(part, g.chip(q, g.a, g.b), self.SPREAD, finish, *only)

    def both(self, axis, k, act):
        p, n = self.g.place(axis)
        pl.when(p >= k)(lambda: act(p - k, axis + "+"))
        pl.when(p + k < n)(lambda: act(p + k, axis + "-"))

    def along_a(self, q, finish=False):
        g = self.g

        def take(a, way):
            t = g.chip(q, a, g.b)
            for part in self.PARTS:
                self.wait(part, t, finish)
                self.onward(part, t, (way, "b+", "b-", "s"), finish)

        for k in range(1, g.na):
            self.both("a", k, take)

    def along_b(self, q, finish=False):
        g = self.g

        def row(b, way):
            def body(i, _):
                t = g.chip(q, lax.rem(g.a + i, g.na), b)
                for part in self.PARTS:
                    self.wait(part, t, finish)
                    self.onward(part, t, (way, "s"), finish)
                return 0

            lax.fori_loop(0, g.na, body, 0)

        for k in range(1, g.nb):
            self.both("b", k, row)

    def first(self, finish=False):
        below, above = self.below, jnp.logical_not(self.below)
        self.column(self.high[0], False, finish, above)
        for q in self.low:
            self.column(q, True, finish)
        self.spread(self.high[0], finish, above)
        self.column(self.high[0], False, finish, below)
        for q in self.low:
            self.along_a(q, finish)
        for q in self.high[1:]:
            self.column(q, False, finish)
        for q in self.low:
            self.along_b(q, finish)
        self.spread(self.high[0], finish, below)
        for q in self.high[1:]:
            self.spread(q, finish)

    def from_sibling(self, upper):
        g = self.g
        count = g.chips // 2

        def body(i, _):
            for part in self.PARTS:
                t = upper * count + i
                arrived(self.piece(part, t, 1 - g.core), self.sib_recv.at[part, t])
            return 0

        lax.fori_loop(0, count, body, 0)


def head_kernel(head_size, up_own, down_own, sq_own, small_in, x_in, cot_in, len_in, coarse_ref, fine_ref,
                ud_full, sq_full, small_ref, x_ref, cot_ref, len_ref,
                x1_ref, a1_ref, h1_ref, s1_ref, a2_ref, heads_ref, pos_ref, att_ref, prob_hbm,
                own, sbuf, up, down, wqkv, wpos, mine, prob_buf,
                move_send, move_recv, local_sem, swap_sem, recv_sem, sib_recv, gather_send, s_send, s_recv,
                load_sem, send_sem, heads_recv, prob_sem):
    g = Grid()
    z, nz, c = g.t, g.nz, g.core
    rows, width = x_in.shape
    cols = width // nz
    units = up.shape[0]
    half = up_own.shape[0]
    me = g.chip(g.z, g.a, g.b)
    own[0] = up_own[...].astype(BF)
    own[1] = down_own[...].astype(BF)
    own[2] = sq_own[...].astype(BF)
    here = pl.ds(me * 2 * half + c * half, half)
    local = [
        pltpu.make_async_copy(own.at[c], ud_full.at[c, here], local_sem.at[0]),
        pltpu.make_async_copy(own.at[2], sq_full.at[me, c], local_sem.at[1]),
    ]
    for copy in local:
        copy.start()
    greet_lines(g, "cabz", g.owner())
    swap = remote(own.at[1 - c], ud_full.at[1 - c, here], swap_sem.at[0], swap_sem.at[1], g.sibling())
    swap.start()
    moves = [
        remote(src, dst, move_send.at[k], move_recv.at[k], g.worker())
        for k, (src, dst) in enumerate(((x_in, x_ref), (len_in, len_ref), (cot_in, cot_ref)))
    ]

    @pl.when(jnp.logical_not(g.at_home()))
    def _():
        for copy in moves[:2]:
            copy.start()

    @pl.when(g.at_home())
    def _():
        x_ref[...] = x_in[...]
        len_ref[...] = len_in[...]
        cot_ref[...] = cot_in[...]

    meeting = Meeting(g, sbuf, s_send, s_recv)
    meeting.start(0, small_in[...].astype(BF))
    gather = Gather(g, ud_full, sq_full, recv_sem, sib_recv, gather_send)
    for copy in local:
        copy.wait()
    swap.wait_recv()
    meeting.start(1, meeting.total(0))
    meeting.start(2, meeting.total(1))
    gather.first()
    meeting.start(3, meeting.total(2))

    @pl.when(jnp.logical_not(g.at_home()))
    def _():
        moves[2].start()
        for copy in moves[:2]:
            copy.wait()

    gather.from_sibling(0)
    loads = [
        pltpu.make_async_copy(ud_full.at[0, pl.ds(0, units)], up, load_sem.at[0]),
        pltpu.make_async_copy(ud_full.at[1, pl.ds(0, units)], down, load_sem.at[1]),
    ]
    per = width // (2 * half)
    squares = pltpu.make_async_copy(sq_full.at[pl.ds(0, 3 * per)], wqkv, load_sem.at[2])
    pieces = cols // half
    positions = [
        pltpu.make_async_copy(
            sq_full.at[3 * per + (z * pieces + i) // 2, (z * pieces + i) % 2],
            wpos.at[pl.ds(i * half, half)],
            load_sem.at[3],
        )
        for i in range(pieces)
    ]
    for load in loads + [squares]:
        load.start()
    for load in positions:
        load.start()
        load.wait()
    small_ref[...] = meeting.total(3).astype(F32)
    gains = small_ref[...]
    signal = x_ref[...].astype(F32)
    normed1 = norm_forward(signal, gains, 0)
    a1_ref[...] = normed1
    for load in loads:
        load.wait()
    resid1 = signal + 0.5 * module_forward(normed1, up, down, h1_ref, s1_ref)
    x1_ref[...] = resid1
    gather.along_a(gather.high[0])
    normed2 = norm_forward(resid1, gains, 1)
    a2_ref[...] = normed2
    squares.wait()
    for k in range(3):
        weight = wqkv[pl.ds(k * per, per)].reshape(width, width)
        out = dot(normed2, weight, NT).astype(BF)
        for q in range(nz):
            mine[q, k] = out[:, q * cols : (q + 1) * cols]
    sends = []
    for k in range(1, nz):
        q = lax.rem(z + k, nz)
        copy = remote(mine.at[q], heads_ref.at[:, pl.ds(z * rows, rows)], send_sem.at[k], heads_recv.at[z], g.time(q))
        copy.start()
        sends.append(copy)
    slot = pl.ds(pl.multiple_of(z * rows, rows), rows)
    for k in range(3):
        heads_ref[k, slot, :] = mine[z, k]
    for q in gather.high[1:]:
        gather.along_a(q)
    fine = fine_ref.shape[1]
    weight = wpos[...]

    def position(i, _):
        table = coarse_ref[0, pl.ds(i, 1), :] * fine_ref[0] + coarse_ref[1, pl.ds(i, 1), :] * fine_ref[1]
        there = pl.ds(pl.multiple_of(i * fine, fine), fine)
        pos_ref[there, :] = dot(table.astype(BF), weight, NT).astype(BF)
        return 0

    lax.fori_loop(0, coarse_ref.shape[1], position, 0)
    for k in range(1, nz):
        q = lax.rem(z + k, nz)
        arrived(heads_ref.at[:, pl.ds(q * rows, rows)], heads_recv.at[q])
    bias = small_ref[10:12, pl.ds(pl.multiple_of(z * cols, cols), cols)]

    def keep(i):
        return pltpu.make_async_copy(
            prob_buf.at[i % 2], prob_hbm.at[:, pl.ds(i * rows, rows)], prob_sem.at[i % 2]
        )

    def attend(i, _):
        pl.when(i >= 2)(lambda: keep(i - 2).wait())
        there = pl.ds(pl.multiple_of(i * rows, rows), rows)
        att_ref[there, :] = attend_block(
            head_size, i, heads_ref[0, there, :], heads_ref.at[1], heads_ref.at[2], pos_ref, bias, len_ref, prob_buf.at[i % 2]
        )
        keep(i).start()
        for k, q in enumerate(gather.high):
            pl.when(i == min(2 * k + 1, nz - 1))(lambda: gather.along_b(q))
        return 0

    lax.fori_loop(0, nz, attend, 0)
    gather.from_sibling(1)
    keep(nz - 2).wait()
    keep(nz - 1).wait()
    swap.wait_send()
    for copy in sends + meeting.sends:
        copy.wait_send()
    gather.first(True)
    for q in gather.high:
        gather.along_a(q, True)
        gather.along_b(q, True)

    @pl.when(jnp.logical_not(g.at_home()))
    def _():
        moves[2].wait()


def head(upward, downward, square, small, signal, cotangent, length, coarse, fine, head_size):
    rows, width = signal.shape
    nz, nf = lax.axis_size("seq"), lax.axis_size("fsdp")
    devices = nz * nf
    chips, plane = devices // 2, nf // 2
    own = upward.shape[0]
    frames, cols = rows * nz, width // nz
    units = own * devices // 2
    heads = cols // head_size
    side = math.isqrt(plane)
    most = max(nz, side if side * side == plane else plane, 2)
    vmem = pl.BlockSpec(memory_space=pltpu.VMEM)
    hbm = pl.BlockSpec(memory_space=pl.ANY)
    shape = jax.ShapeDtypeStruct
    dma = pltpu.SemaphoreType.DMA
    return pl.pallas_call(
        lambda *refs: head_kernel(head_size, *refs),
        name="head",
        out_shape=(
            shape((2, devices * own, width), BF),
            shape((chips, 2, own, width), BF),
            shape(small.shape, F32),
            shape(signal.shape, signal.dtype),
            shape(cotangent.shape, cotangent.dtype),
            shape(length.shape, length.dtype),
            shape((rows, width), F32),
            shape((rows, width), BF),
            shape((rows, units), BF),
            shape((rows, units), BF),
            shape((rows, width), BF),
            shape((3, frames, cols), BF),
            shape((2 * frames, cols), BF),
            shape((frames, cols), BF),
            shape((heads, frames, frames), BF),
        ),
        in_specs=[vmem] * 9,
        out_specs=[hbm] * 2 + [vmem] * 12 + [hbm],
        scratch_shapes=[
            pltpu.VMEM((3, own, width), BF),
            pltpu.VMEM((4, most) + small.shape, BF),
            pltpu.VMEM((units, width), BF),
            pltpu.VMEM((units, width), BF),
            pltpu.VMEM((3 * width // (2 * own), 2, own, width), BF),
            pltpu.VMEM((cols, width), BF),
            pltpu.VMEM((nz, 3, rows, cols), BF),
            pltpu.VMEM((2, heads, rows, frames), BF),
            dma((3,)),
            dma((3,)),
            dma((2,)),
            dma((2,)),
            dma((3, chips)),
            dma((3, chips)),
            dma((7, 3, chips)),
            dma((4, most)),
            dma((4, most)),
            dma((4,)),
            dma((nz,)),
            dma((nz,)),
            dma((2,)),
        ],
        compiler_params=pltpu.CompilerParams(
            collective_id=5, has_side_effects=True, vmem_limit_bytes=56 * 1024 * 1024
        ),
    )(upward, downward, square, small, signal, cotangent, length, coarse, fine)


def per_device(
    inputs,
    cotangent,
    lengths,
    square,
    upward,
    downward,
    vectors,
    kernel,
    square_momentum,
    square_variance,
    upward_momentum,
    upward_variance,
    downward_momentum,
    downward_variance,
    vectors_momentum,
    vectors_variance,
    kernel_momentum,
    kernel_variance,
):
    model_width = inputs.shape[2]
    seq_place = lax.axis_index("seq")
    seq_frames = inputs.shape[1] * lax.axis_size("seq")
    head_size = D // H
    coarse, fine = position_tables(seq_frames, model_width)
    place = seq_place * lax.axis_size("fsdp") + lax.axis_index("fsdp")
    share = vectors.shape[1]
    tall = -(-(vectors.shape[0] + kernel.shape[0]) // 16) * 16
    small = jnp.concatenate([vectors, kernel], axis=0)
    small = lax.dynamic_update_slice(jnp.zeros((tall, model_width), F32), small, (0, place * share))
    length = jnp.broadcast_to(lengths.astype(F32)[:, None], (8, LANES))
    (
        full_ud, full_sq, small, signal, cotangent_here, length,
        resid1, normed1, hidden1, active1, normed2, heads, pos_heads, attended, prob,
    ) = head(upward, downward, square, small, inputs[0], cotangent[0], length, coarse, fine, head_size)
    full_sq = full_sq.reshape(model_width * 8, model_width)
    (
        layer_output, grad_res2, grad_out_head, out_time, grad_att_b, normed3, grad_pair, grad_conv_b, swish_b, normed4,
        active4, grad_hidden4, half4, small_grads, grad_taps,
    ) = middle(length, attended, resid1, cotangent_here, small, kernel.shape[0], full_ud, full_sq)
    layer_output = layer_output[None]
    input_grad, matrix_grads, square_grad, small_sums = back(
        heads, pos_heads, grad_out_head, prob, head_size, coarse, fine, small,
        signal, resid1, grad_res2, (normed1, hidden1, active1, normed2), (normed4, active4, grad_hidden4, half4),
        (out_time, grad_att_b, normed3, grad_pair, grad_conv_b, swish_b), small_grads, grad_taps, full_ud, full_sq,
    )
    input_grad = input_grad[None]
    upward_grad, downward_grad = matrix_grads[0], matrix_grads[1]
    small_own = lax.dynamic_slice_in_dim(small_sums, place * share, share, 1)
    vectors_grad = small_own[: vectors.shape[0]]
    kernel_grad = small_own[vectors.shape[0] : vectors.shape[0] + kernel.shape[0]]
    square_next, momentum_square, variance_square = adam_step(
        square, square_grad, square_momentum, square_variance, DECAY_RATE
    )
    upward_next, momentum_upward, variance_upward = adam_step(
        upward, upward_grad, upward_momentum, upward_variance, DECAY_RATE
    )
    downward_next, momentum_downward, variance_downward = adam_step(
        downward, downward_grad, downward_momentum, downward_variance, DECAY_RATE
    )
    vectors_next, momentum_vectors, variance_vectors = adam_step(
        vectors, vectors_grad, vectors_momentum, vectors_variance, 0.0
    )
    kernel_next, momentum_kernel, variance_kernel = adam_step(
        kernel, kernel_grad, kernel_momentum, kernel_variance, DECAY_RATE
    )
    return (
        layer_output,
        input_grad,
        square_grad,
        upward_grad,
        downward_grad,
        vectors_grad,
        kernel_grad,
        square_next,
        upward_next,
        downward_next,
        vectors_next,
        kernel_next,
        momentum_square,
        variance_square,
        momentum_upward,
        variance_upward,
        momentum_downward,
        variance_downward,
        momentum_vectors,
        variance_vectors,
        momentum_kernel,
        variance_kernel,
    )


def solution(mesh):
    return jax.shard_map(
        per_device,
        mesh=mesh,
        in_specs=(
            P("fsdp", "seq", None),
            P("fsdp", "seq", None),
            P("fsdp"),
            P(("seq", "fsdp"), None),
            P(("seq", "fsdp"), None),
            P(("seq", "fsdp"), None),
            P(None, ("seq", "fsdp")),
            P(None, ("seq", "fsdp")),
            P(("seq", "fsdp"), None),
            P(("seq", "fsdp"), None),
            P(("seq", "fsdp"), None),
            P(("seq", "fsdp"), None),
            P(("seq", "fsdp"), None),
            P(("seq", "fsdp"), None),
            P(None, ("seq", "fsdp")),
            P(None, ("seq", "fsdp")),
            P(None, ("seq", "fsdp")),
            P(None, ("seq", "fsdp")),
        ),
        out_specs=(
            P("fsdp", "seq", None),
            P("fsdp", "seq", None),
            P(("seq", "fsdp"), None),
            P(("seq", "fsdp"), None),
            P(("seq", "fsdp"), None),
            P(None, ("seq", "fsdp")),
            P(None, ("seq", "fsdp")),
            P(("seq", "fsdp"), None),
            P(("seq", "fsdp"), None),
            P(("seq", "fsdp"), None),
            P(None, ("seq", "fsdp")),
            P(None, ("seq", "fsdp")),
            P(("seq", "fsdp"), None),
            P(("seq", "fsdp"), None),
            P(("seq", "fsdp"), None),
            P(("seq", "fsdp"), None),
            P(("seq", "fsdp"), None),
            P(("seq", "fsdp"), None),
            P(None, ("seq", "fsdp")),
            P(None, ("seq", "fsdp")),
            P(None, ("seq", "fsdp")),
            P(None, ("seq", "fsdp")),
        ),
        check_vma=False,
    )
```

profile of v0, /device:TPU:0, one launch (start us, length us, event | category | flops | bytes accessed | tf_op | source)
XLA Modules:
  0.0 262.5 jit_solution(14380012682501647934)
XLA Ops:
  0.7 0.8 copy.68
  1.4 0.7 pad_maximum_fusion.2
  2.2 0.8 dynamic_update_slice.3.refs_3_
  3.0 0.0 copy-start.5
  3.6 0.6 broadcast_in_dim.37.refs_6_
  4.3 0.3 fusion.4
  4.6 0.7 pad_maximum_fusion.1.refs_7_.refs_3_
  5.3 0.5 multiply_cosine_fusion
  5.8 0.7 pad_maximum_fusion.refs_8_.refs_4_
  6.5 0.0 copy-done.5
  6.5 96.0 %head.1 = (bf16[2,4096,512]{2,1,0:T(8,128)(2,1)}, bf16[16,2,128,512]{3,2,1,0:T(8,128)(2,1)}, f32[48,512]{1,0:T(8,128)}, bf16[256,512]{1,0:T(8,128)(2,1)}, bf16[2...) custom-call(f32[128,512]{1,0:T(8,128)} %refs_0_.1, ...), custom_call_target="tpu_custom_call" | custom-call | tf_op jit(solution)/shard_map/head/pallas_call | solution.py:1298
  102.5 53.9 %middle.1 = (bf16[256,512]{1,0:T(8,128)(2,1)}, f32[256,512]{1,0:T(8,128)}, bf16[1024,128]{1,0:T(8,128)(2,1)}, bf16[256,512]{1,0:T(8,128)(2,1)}, bf16[256,512]{1,...) custom-call(f32[8,128]{1,0:T(8,128)} %get-tuple-element.56.refs_0_, ...), custom_call_target="tpu_custom_call" | custom-call | tf_op jit(solution)/shard_map/middle/pallas_call | solution.py:493
  156.4 0.0 copy-start
  156.4 0.0 copy-start.1
  156.4 0.0 copy-start.2
  156.4 0.0 copy-start.6
  156.4 0.0 copy-start.7
  156.5 0.0 copy-start.8
  156.5 0.0 copy-start.9
  156.5 0.0 copy-start.10
  156.5 0.0 copy-start.11
  156.5 95.5 %back.1 = (f32[256,512]{1,0:T(8,128)}, f32[2,128,512]{2,1,0:T(8,128)}, f32[128,512]{1,0:T(8,128)}, f32[48,512]{1,0:T(8,128)}) custom-call(bf16[3,1024,128]{2,1,0:T(8,128)(2,1)} %get-tuple-element.64.refs_0_, bf16[2048,128]{1,0:T(8,128)(2,1)} %get-tuple-element.65.refs_1_, bf16[1024,128]{1,0:T(8,128)(2,1)} %get-tuple-element.66.refs_2_, ...), custom_call_target="tpu_custom_call" | custom-call | tf_op jit(solution)/shard_map/back/pallas_call | solution.py:936
  252.0 0.0 copy-start.13
  252.1 0.0 copy-start.16
  252.1 0.0 copy-start.17
  252.1 0.0 copy-start.14
  252.1 0.0 copy-start.15
  252.1 0.0 copy-start.12
  252.1 0.0 copy-start.4
  252.1 0.0 copy-start.3
  252.1 0.0 copy-done
  252.1 0.0 copy-done.1
  252.2 0.0 copy-done.2
  252.2 0.0 copy-done.6
  252.2 0.0 copy-done.7
  252.2 0.0 copy-done.8
  252.2 0.0 copy-done.9
  252.2 0.0 copy-done.10
  252.2 0.0 copy-done.11
  252.2 3.0 %multiply_subtract_fusion = (f32[128,512]{1,0:T(8,128)}, f32[128,512]{1,0:T(8,128)}, f32[128,512]{1,0:T(8,128)}, f32[128,512]{1,0:T(8,128)}, f32[128,512]{1,0:T(...) fusion(f32[128,512]{1,0:T(8,128)S(1)} %copy-done.1, ...), kind=kLoop, calls=%fused_computation.7 | loop fusion | flops 2949120 | bytes 6029312 | tf_op jit(solution)/shard_map/sub | solution.py:44
  255.2 0.0 copy-done.13
  255.2 0.0 copy-done.16
  255.2 0.0 copy-done.17
  255.2 1.4 multiply_subtract_fusion.4
  256.6 0.0 copy-done.14
  256.6 0.1 copy.69
  256.7 0.0 copy-done.15
  256.7 0.1 copy.71
  256.8 0.8 multiply_subtract_fusion.3
  257.6 0.7 copy.74
  258.3 0.7 copy.75
  259.0 0.7 copy.76
  259.6 0.7 copy.77
  260.3 0.0 copy-done.12
  260.3 0.7 copy.83
  261.0 0.0 copy-done.4
  261.0 0.8 copy.84
  261.8 0.0 copy-done.3
  261.8 0.7 copy.85
  (5 shorter events, 0.0 us)
Async XLA Ops:
  3.0 3.5 %copy-start.5 = (f32[48,512]{1,0:T(8,128)}, f32[48,512]{1,0:T(8,128)S(1)}, u32[]{:S(2)}) copy-start(f32[48,512]{1,0:T(8,128)S(1)} %dynamic_update_slice.3.refs_3_) | copy-start | bytes 294916
  156.4 95.7 %copy-start = (f32[128,512]{1,0:T(8,128)S(1)}, f32[128,512]{1,0:T(8,128)}, u32[]{:S(2)}) copy-start(f32[128,512]{1,0:T(8,128)} %refs_0_.1) | copy-start | bytes 786436
  156.4 95.7 %copy-start.1 = (f32[128,512]{1,0:T(8,128)S(1)}, f32[128,512]{1,0:T(8,128)}, u32[]{:S(2)}) copy-start(f32[128,512]{1,0:T(8,128)} %refs_1_.1) | copy-start | bytes 786436
  156.4 95.7 %copy-start.2 = (f32[128,512]{1,0:T(8,128)S(1)}, f32[128,512]{1,0:T(8,128)}, u32[]{:S(2)}) copy-start(f32[128,512]{1,0:T(8,128)} %refs_2_.1) | copy-start | bytes 786436
  156.4 95.7 %copy-start.6 = (f32[128,512]{1,0:T(8,128)S(1)}, f32[128,512]{1,0:T(8,128)}, u32[]{:S(2)}) copy-start(f32[128,512]{1,0:T(8,128)} %param.30) | copy-start | bytes 786436
  156.4 95.7 %copy-start.7 = (f32[128,512]{1,0:T(8,128)S(1)}, f32[128,512]{1,0:T(8,128)}, u32[]{:S(2)}) copy-start(f32[128,512]{1,0:T(8,128)} %param.31) | copy-start | bytes 786436
  156.5 95.7 %copy-start.8 = (f32[128,512]{1,0:T(8,128)S(1)}, f32[128,512]{1,0:T(8,128)}, u32[]{:S(2)}) copy-start(f32[128,512]{1,0:T(8,128)} %param.29) | copy-start | bytes 786436
  156.5 95.7 %copy-start.9 = (f32[128,512]{1,0:T(8,128)S(1)}, f32[128,512]{1,0:T(8,128)}, u32[]{:S(2)}) copy-start(f32[128,512]{1,0:T(8,128)} %param.28) | copy-start | bytes 786436
  156.5 95.7 %copy-start.10 = (f32[128,512]{1,0:T(8,128)S(1)}, f32[128,512]{1,0:T(8,128)}, u32[]{:S(2)}) copy-start(f32[128,512]{1,0:T(8,128)} %param.27) | copy-start | bytes 786436
  156.5 95.7 %copy-start.11 = (f32[128,512]{1,0:T(8,128)S(1)}, f32[128,512]{1,0:T(8,128)}, u32[]{:S(2)}) copy-start(f32[128,512]{1,0:T(8,128)} %param.26) | copy-start | bytes 786436
  252.0 3.1 %copy-start.13 = (f32[14,16]{1,0:T(8,128)S(1)}, f32[14,16]{1,0:T(8,128)}, u32[]{:S(2)}) copy-start(f32[14,16]{1,0:T(8,128)} %param.24) | copy-start | bytes 2692
  252.1 3.1 %copy-start.16 = (f32[14,16]{1,0:T(8,128)S(1)}, f32[14,16]{1,0:T(8,128)}, u32[]{:S(2)}) copy-start(f32[14,16]{1,0:T(8,128)} %param.32) | copy-start | bytes 2692
  252.1 3.1 %copy-start.17 = (f32[14,16]{1,0:T(8,128)S(1)}, f32[14,16]{1,0:T(8,128)}, u32[]{:S(2)}) copy-start(f32[14,16]{1,0:T(8,128)} %param.33) | copy-start | bytes 2692
  252.1 4.5 %copy-start.14 = (f32[31,16]{0,1:T(8,128)S(1)}, f32[31,16]{0,1:T(8,128)}, u32[]{:S(2)}) copy-start(f32[31,16]{0,1:T(8,128)} %param.34) | copy-start | bytes 5956
  252.1 4.6 %copy-start.15 = (f32[31,16]{0,1:T(8,128)S(1)}, f32[31,16]{0,1:T(8,128)}, u32[]{:S(2)}) copy-start(f32[31,16]{0,1:T(8,128)} %param.35) | copy-start | bytes 5956
  252.1 8.2 %copy-start.12 = (bf16[256,512]{1,0:T(8,128)(2,1)S(1)}, bf16[256,512]{1,0:T(8,128)(2,1)}, u32[]{:S(2)}) copy-start(bf16[256,512]{1,0:T(8,128)(2,1)} %get-tuple-element.63) | copy-start | bytes 786436
  252.1 8.9 %copy-start.4 = (f32[256,512]{1,0:T(8,128)S(1)}, f32[256,512]{1,0:T(8,128)}, u32[]{:S(2)}) copy-start(f32[256,512]{1,0:T(8,128)} %get-tuple-element.86) | copy-start | bytes 1572868
  252.1 9.7 %copy-start.3 = (f32[128,512]{1,0:T(8,128)S(1)}, f32[128,512]{1,0:T(8,128)}, u32[]{:S(2)}) copy-start(f32[128,512]{1,0:T(8,128)} %get-tuple-element.232) | copy-start | bytes 786436
where the time goes:
time: 263 us
  Pallas kernels  245 us (93%)
  other arithmetic  8.15 us (3%)
  local copies, waits for them, and re-layouts  7.38 us (3%)
    pallas_call x1, Pallas kernels, head(): pl.pallas_call(lambda *refs: head_kernel(head_size, *refs), name='head',...  96 us
    pallas_call x1, Pallas kernels, back(): pl.pallas_call(lambda *refs: back_kernel(head_size, *refs), name='back',...  95.5 us
    pallas_call x1, Pallas kernels, middle(): pl.pallas_call(lambda *refs: middle_kernel(taps, *refs), name='middle', o...  53.9 us
    unnamed x46, local copies, waits for them, and re-layouts  5.96 us

commit v1 on v0

--- a/solution.py
+++ b/solution.py
@@ -33,15 +33,6 @@
     with_cosine = jnp.where(even, sine, cosine)
     with_sine = jnp.where(even, -cosine, sine)
     return jnp.stack([with_cosine, with_sine]), jnp.stack([jnp.cos(fine_phase), jnp.sin(fine_phase)])
-
-
-def adam_step(weight, gradient, first_mom, second_mom, decay):
-    first_new = BETA_ONE * first_mom + (1.0 - BETA_ONE) * gradient
-    second_new = BETA_TWO * second_mom + (1.0 - BETA_TWO) * gradient * gradient
-    fix_one = 1.0 - BETA_ONE**ADAM_STEP
-    fix_two = 1.0 - BETA_TWO**ADAM_STEP
-    update = first_new / fix_one / (jnp.sqrt(second_new / fix_two) + ADAM_EPS)
-    return (weight - LEARN_RATE * (update + decay * weight), first_new, second_new)
 
 
 MESH = pl.DeviceIdType.MESH
@@ -548,22 +539,29 @@
 
 
 class Meeting:
-    def __init__(self, g, buf, send_sem, recv_sem):
-        self.g, self.buf, self.send_sem, self.recv_sem = g, buf, send_sem, recv_sem
-        self.sends = []
+    def __init__(self, g, buf, send_sem, recv_sem, order="cabz"):
+        self.g, self.buf, self.send_sem, self.recv_sem, self.order = g, buf, send_sem, recv_sem, order
+
+    def copies(self, level):
+        p, n, device = self.g.line(self.order[level])
+        here = self.buf.at[level, p]
+        return [
+            remote(here, here, self.send_sem.at[level, k], self.recv_sem.at[level, p], device(lax.rem(p + k, n)))
+            for k in range(1, n)
+        ]
 
     def start(self, level, value):
-        axis = "cabz"[level]
-        p, n, device = self.g.line(axis)
-        self.buf[level, p] = value
-        for k in range(1, n):
-            here = self.buf.at[level, p]
-            copy = remote(here, here, self.send_sem.at[level, k], self.recv_sem.at[level, p], device(lax.rem(p + k, n)))
+        self.buf[level, self.g.line(self.order[level])[0]] = value
+        for copy in self.copies(level):
             copy.start()
-            self.sends.append(copy)
+
+    def finish(self):
+        for level in range(len(self.order)):
+            for copy in self.copies(level):
+                copy.wait_send()
 
     def total(self, level):
-        p, n, _ = self.g.line("cabz"[level])
+        p, n, _ = self.g.line(self.order[level])
         for k in range(1, n):
             q = lax.rem(p + k, n)
             arrived(self.buf.at[level, q], self.recv_sem.at[level, q])
@@ -703,7 +701,7 @@
                 a4_ref, s4_ref, gh4_ref, e4_ref, o_ref, e2_ref, a3_ref, gpair_ref, e3_ref, sw_ref, some_ref, gtaps_ref,
                 prob_hbm, ud_hbm, sq_hbm,
                 gx_ref, ud_out, sq_out, small_out,
-                prob_buf, gk_acc, gv_acc, gpos_acc, gbias, grads, prob_sem, wqkv, heads, gqkv, gh1, small, gud, gsq, sib_ud, sib_sq, rb, ra, rz, sbuf, fin_send_buf, fin, gx_buf, gx_in, gx_sem,
+                prob_buf, gk_acc, gv_acc, gpos_acc, gbias, grads, prob_sem, wqkv, heads, gqkv, gh1, small, few, fbuf, f_send, f_recv, gud, gsq, sib_ud, sib_sq, rb, ra, rz, sbuf, fin_send_buf, fin, gx_buf, gx_in, gx_sem,
                 load_sem, h_send, h_recv, sib_send, sib_recv, b_send, b_recv, a_send, a_recv, z_send, z_recv, s_send, s_recv,
                 fin_send, fin_recv):
     g = Grid()
@@ -727,6 +725,11 @@
         load.start()
     greet_lines(g, "cabz", g.worker())
     sends = []
+    small[...] = jnp.zeros_like(small)
+    small[0:8, :] = some_ref[...]
+    small[8 : 8 + gtaps_ref.shape[0], :] = gtaps_ref[...]
+    early = Meeting(g, sbuf, s_send, s_recv)
+    early.start(0, small[...])
     red = Reduction(
         g, gud, gsq, sib_ud, sib_sq, (sib_send, sib_recv), rb, ra, rz,
         {"b": (b_send, b_recv), "a": (a_send, a_recv), "z": (z_send, z_recv)},
@@ -757,9 +760,11 @@
     square_terms(5, gpair_ref[0], a3_ref[...])
     square_terms(4, e2_ref[...], o_ref[...])
     red.to_sibling(high, 0)
+    early.start(1, early.total(0))
     matrix_terms(0, gh4_ref, a4_ref[...], units, units)
     matrix_terms(1, s4_ref, e4_ref[...], units, units)
     red.to_sibling(high, 1)
+    early.start(2, early.total(1))
     gk_acc[...] = jnp.zeros_like(gk_acc)
     gv_acc[...] = jnp.zeros_like(gv_acc)
     gpos_acc[...] = jnp.zeros_like(gpos_acc)
@@ -778,6 +783,7 @@
 
         @pl.when(i == 0)
         def _():
+            early.start(3, early.total(2))
             red.from_sibling(high, 0)
             red.along("b", high, 0)
 
@@ -790,6 +796,7 @@
         return 0
 
     lax.fori_loop(0, nz, attend, 0)
+    small[...] = early.total(3)
     grads_k = gk_acc[...].T.astype(BF)
     grads_v = gv_acc[...].T.astype(BF)
     for q in range(nz):
@@ -850,17 +857,14 @@
     gx_buf[...] = (grad1 + grad_add).astype(BF)
     home = remote(gx_buf, gx_in, gx_sem.at[0], gx_sem.at[1], g.owner())
     pl.when(away)(lambda: home.start())
-    small[...] = jnp.zeros_like(small)
-    small[0:1, :] = gain0
-    small[1:2, :] = shift0
-    small[2:3, :] = gain1
-    small[3:4, :] = shift1
-    small[4:10, :] = some_ref[0:6, :]
-    small[10:12, pl.ds(pl.multiple_of(z * cols, cols), cols)] = gbias[...]
-    small[12:14, :] = some_ref[6:8, :]
-    small[14 : 14 + gtaps_ref.shape[0], :] = gtaps_ref[...]
-    meeting = Meeting(g, sbuf, s_send, s_recv)
-    meeting.start(0, small[...])
+    few[...] = jnp.zeros_like(few)
+    few[0:1, :] = gain0
+    few[1:2, :] = shift0
+    few[2:3, :] = gain1
+    few[3:4, :] = shift1
+    few[4:6, pl.ds(pl.multiple_of(z * cols, cols), cols)] = gbias[...]
+    meeting = Meeting(g, fbuf, f_send, f_recv)
+    meeting.start(0, few[...])
     red.from_sibling(low, 1)
     red.along("b", low, 1)
     red.along("b", low, 2)
@@ -887,7 +891,11 @@
     swap.start()
     ud_out[c] = gud[c, at(c), :].astype(F32)
     sq_out[...] = gsq[me, c].astype(F32)
-    small_out[...] = meeting.total(3)
+    total = meeting.total(3)
+    small_out[0:4, :] = total[0:4]
+    small_out[4:10, :] = small[0:6, :]
+    small_out[10:12, :] = total[4:6]
+    small_out[12 : small.shape[0] + 6, :] = small[6:, :]
     for planes in (high, low):
         for part in range(3):
             for axis in "baz":
@@ -895,8 +903,10 @@
         for kind in range(2):
             for q in planes:
                 red.sibling_copy(q, kind).wait_send()
-    for copy in sends + meeting.sends:
+    for copy in sends:
         copy.wait_send()
+    early.finish()
+    meeting.finish()
 
     @pl.when(away)
     def _():
@@ -923,7 +933,7 @@
     own = ud_full.shape[1] // (2 * chips)
     block = 3 * own
     most = max(nz, na, nb, 2)
-    tall = -(-(14 + gtaps.shape[0]) // 8) * 8
+    tall = -(-(8 + gtaps.shape[0]) // 8) * 8
     vmem = pl.BlockSpec(memory_space=pltpu.VMEM)
     hbm = pl.BlockSpec(memory_space=pl.ANY)
     shape = jax.ShapeDtypeStruct
@@ -940,7 +950,7 @@
             shape((rows, width), F32),
             shape((2, own, width), F32),
             shape((own, width), F32),
-            shape((tall, width), F32),
+            shape((tall + 6, width), F32),
         ),
         in_specs=[vmem] * len(operands) + [hbm] * 3,
         out_specs=[vmem] * 4,
@@ -957,6 +967,10 @@
             pltpu.VMEM((3, rows, width), BF),
             pltpu.VMEM((rows, units), BF),
             pltpu.VMEM((tall, width), F32),
+            pltpu.VMEM((8, width), F32),
+            pltpu.VMEM((4, most, 8, width), F32),
+            dma((4, most)),
+            dma((4, most)),
             pltpu.VMEM((2, 2 * units, width), BF),
             pltpu.VMEM((chips, 2, own, width), BF),
             pltpu.VMEM((2 * units, width), BF),
@@ -992,6 +1006,51 @@
     )(*operands, prob, ud_full, sq_full)
 
 
+def finish_kernel(rows, y_ref, gx_ref, matrices_ref, square_ref, small_ref, *refs):
+    states, outs = refs[:15], refs[15:]
+    outs[0][...] = y_ref[...]
+    outs[1][...] = gx_ref[...]
+    count, share = rows, states[9].shape[1]
+    taps = states[12].shape[1]
+    width = small_ref.shape[1]
+    place = lax.axis_index("seq") * lax.axis_size("fsdp") + lax.axis_index("fsdp")
+    own = pltpu.roll(small_ref[...], lax.rem(width - place * share, width), 1)[:, :LANES]
+    below = jnp.concatenate([own[count : count + taps], jnp.zeros((-taps % 8, LANES), F32)], axis=0)
+    gradients = (
+        square_ref[...],
+        matrices_ref[0],
+        matrices_ref[1],
+        own[:count, :share],
+        below.T[:share, :taps],
+    )
+    fix_one = 1.0 - BETA_ONE**ADAM_STEP
+    fix_two = 1.0 - BETA_TWO**ADAM_STEP
+    for k, gradient in enumerate(gradients):
+        weight, first_mom, second_mom = (ref[...] for ref in states[3 * k : 3 * k + 3])
+        decay = 0.0 if k == 3 else DECAY_RATE
+        first_new = BETA_ONE * first_mom + (1.0 - BETA_ONE) * gradient
+        second_new = BETA_TWO * second_mom + (1.0 - BETA_TWO) * gradient * gradient
+        update = first_new / fix_one / (jnp.sqrt(second_new / fix_two) + ADAM_EPS)
+        there = outs[2 + 4 * k : 6 + 4 * k]
+        there[0][...] = gradient
+        there[1][...] = weight - LEARN_RATE * (update + decay * weight)
+        there[2][...] = first_new
+        there[3][...] = second_new
+
+
+def finish(layer_output, input_grad, matrices, square, small, states):
+    flat = [array for state in states for array in state]
+    results = [layer_output, input_grad] + [array for state in states for array in (state[0],) * 4]
+    vmem = pl.BlockSpec(memory_space=pltpu.VMEM)
+    return pl.pallas_call(
+        lambda *refs: finish_kernel(states[3][0].shape[0], *refs),
+        name="finish",
+        out_shape=[jax.ShapeDtypeStruct(array.shape, array.dtype) for array in results],
+        in_specs=[vmem] * (5 + len(flat)),
+        out_specs=[vmem] * len(results),
+    )(layer_output, input_grad, matrices, square, small, *flat)
+
+
 def when(*conditions):
     holds = 1
     for condition in conditions:
@@ -1093,19 +1152,29 @@
         for k in range(1, g.nb):
             self.both("b", k, row)
 
+    def own(self, finish=False):
+        if len(self.low) == 2:
+            self.column(self.low[0], True, finish, self.below)
+        self.column(self.high[0], False, finish, jnp.logical_not(self.below))
+
     def first(self, finish=False):
         below, above = self.below, jnp.logical_not(self.below)
-        self.column(self.high[0], False, finish, above)
-        for q in self.low:
+        if len(self.low) == 2:
+            self.column(self.low[0], True, finish, above)
+        else:
+            self.column(self.low[0], True, finish)
+        for q in self.high[1:]:
+            self.column(q, False, finish, above)
+        self.along_a(self.low[0], finish)
+        for q in self.low[1:]:
             self.column(q, True, finish)
+            self.along_a(q, finish)
         self.spread(self.high[0], finish, above)
         self.column(self.high[0], False, finish, below)
         for q in self.low:
-            self.along_a(q, finish)
+            self.along_b(q, finish)
         for q in self.high[1:]:
-            self.column(q, False, finish)
-        for q in self.low:
-            self.along_b(q, finish)
+            self.column(q, False, finish, below)
         self.spread(self.high[0], finish, below)
         for q in self.high[1:]:
             self.spread(q, finish)
@@ -1123,10 +1192,10 @@
         lax.fori_loop(0, count, body, 0)
 
 
-def head_kernel(head_size, up_own, down_own, sq_own, small_in, x_in, cot_in, len_in, coarse_ref, fine_ref,
+def head_kernel(head_size, up_own, down_own, sq_own, vec_in, taps_in, x_in, cot_in, len_smem, coarse_ref, fine_ref,
                 ud_full, sq_full, small_ref, x_ref, cot_ref, len_ref,
                 x1_ref, a1_ref, h1_ref, s1_ref, a2_ref, heads_ref, pos_ref, att_ref, prob_hbm,
-                own, sbuf, up, down, wqkv, wpos, mine, prob_buf,
+                own, len_in, columns, sbuf, up, down, wqkv, wpos, mine, prob_buf,
                 move_send, move_recv, local_sem, swap_sem, recv_sem, sib_recv, gather_send, s_send, s_recv,
                 load_sem, send_sem, heads_recv, prob_sem):
     g = Grid()
@@ -1146,6 +1215,16 @@
     ]
     for copy in local:
         copy.start()
+    len_in[...] = jnp.full(len_in.shape, len_smem[0].astype(F32))
+    share = vec_in.shape[1]
+    count = vec_in.shape[0]
+    taps = taps_in.shape[1]
+    lane = lax.broadcasted_iota(jnp.int32, (share, width), 1)
+    column = lax.broadcasted_iota(jnp.int32, (share, width), 0)
+    place = jnp.where(lane - (g.z * g.nf + g.f) * share == column, 1.0, 0.0).astype(BF)
+    columns[...] = jnp.zeros_like(columns)
+    columns[0:count, :] = dot(vec_in[...].astype(BF), place, NN)
+    columns[count : count + taps, :] = dot(taps_in[...].astype(BF), place, TN)
     greet_lines(g, "cabz", g.owner())
     swap = remote(own.at[1 - c], ud_full.at[1 - c, here], swap_sem.at[0], swap_sem.at[1], g.sibling())
     swap.start()
@@ -1166,11 +1245,12 @@
         cot_ref[...] = cot_in[...]
 
     meeting = Meeting(g, sbuf, s_send, s_recv)
-    meeting.start(0, small_in[...].astype(BF))
+    meeting.start(0, columns[...].astype(BF))
     gather = Gather(g, ud_full, sq_full, recv_sem, sib_recv, gather_send)
     for copy in local:
         copy.wait()
     swap.wait_recv()
+    gather.own()
     meeting.start(1, meeting.total(0))
     meeting.start(2, meeting.total(1))
     gather.first()
@@ -1268,8 +1348,10 @@
     keep(nz - 2).wait()
     keep(nz - 1).wait()
     swap.wait_send()
-    for copy in sends + meeting.sends:
+    for copy in sends:
         copy.wait_send()
+    meeting.finish()
+    gather.own(True)
     gather.first(True)
     for q in gather.high:
         gather.along_a(q, True)
@@ -1280,7 +1362,7 @@
         moves[2].wait()
 
 
-def head(upward, downward, square, small, signal, cotangent, length, coarse, fine, head_size):
+def head(upward, downward, square, vectors, kernel, signal, cotangent, lengths, coarse, fine, head_size):
     rows, width = signal.shape
     nz, nf = lax.axis_size("seq"), lax.axis_size("fsdp")
     devices = nz * nf
@@ -1289,6 +1371,7 @@
     frames, cols = rows * nz, width // nz
     units = own * devices // 2
     heads = cols // head_size
+    tall = -(-(vectors.shape[0] + kernel.shape[1]) // 16) * 16
     side = math.isqrt(plane)
     most = max(nz, side if side * side == plane else plane, 2)
     vmem = pl.BlockSpec(memory_space=pltpu.VMEM)
@@ -1301,10 +1384,10 @@
         out_shape=(
             shape((2, devices * own, width), BF),
             shape((chips, 2, own, width), BF),
-            shape(small.shape, F32),
+            shape((tall, width), F32),
             shape(signal.shape, signal.dtype),
             shape(cotangent.shape, cotangent.dtype),
-            shape(length.shape, length.dtype),
+            shape((8, LANES), F32),
             shape((rows, width), F32),
             shape((rows, width), BF),
             shape((rows, units), BF),
@@ -1315,11 +1398,13 @@
             shape((frames, cols), BF),
             shape((heads, frames, frames), BF),
         ),
-        in_specs=[vmem] * 9,
+        in_specs=[vmem] * 7 + [pl.BlockSpec(memory_space=pltpu.SMEM)] + [vmem] * 2,
         out_specs=[hbm] * 2 + [vmem] * 12 + [hbm],
         scratch_shapes=[
             pltpu.VMEM((3, own, width), BF),
-            pltpu.VMEM((4, most) + small.shape, BF),
+            pltpu.VMEM((8, LANES), F32),
+            pltpu.VMEM((tall, width), F32),
+            pltpu.VMEM((4, most, tall, width), BF),
             pltpu.VMEM((units, width), BF),
             pltpu.VMEM((units, width), BF),
             pltpu.VMEM((3 * width // (2 * own), 2, own, width), BF),
@@ -1343,7 +1428,7 @@
         compiler_params=pltpu.CompilerParams(
             collective_id=5, has_side_effects=True, vmem_limit_bytes=56 * 1024 * 1024
         ),
-    )(upward, downward, square, small, signal, cotangent, length, coarse, fine)
+    )(upward, downward, square, vectors, kernel, signal, cotangent, lengths, coarse, fine)
 
 
 def per_device(
@@ -1367,64 +1452,53 @@
     kernel_variance,
 ):
     model_width = inputs.shape[2]
-    seq_place = lax.axis_index("seq")
     seq_frames = inputs.shape[1] * lax.axis_size("seq")
     head_size = D // H
     coarse, fine = position_tables(seq_frames, model_width)
-    place = seq_place * lax.axis_size("fsdp") + lax.axis_index("fsdp")
-    share = vectors.shape[1]
-    tall = -(-(vectors.shape[0] + kernel.shape[0]) // 16) * 16
-    small = jnp.concatenate([vectors, kernel], axis=0)
-    small = lax.dynamic_update_slice(jnp.zeros((tall, model_width), F32), small, (0, place * share))
-    length = jnp.broadcast_to(lengths.astype(F32)[:, None], (8, LANES))
     (
         full_ud, full_sq, small, signal, cotangent_here, length,
         resid1, normed1, hidden1, active1, normed2, heads, pos_heads, attended, prob,
-    ) = head(upward, downward, square, small, inputs[0], cotangent[0], length, coarse, fine, head_size)
+    ) = head(upward, downward, square, vectors, kernel.T, inputs[0], cotangent[0], lengths, coarse, fine, head_size)
     full_sq = full_sq.reshape(model_width * 8, model_width)
     (
         layer_output, grad_res2, grad_out_head, out_time, grad_att_b, normed3, grad_pair, grad_conv_b, swish_b, normed4,
         active4, grad_hidden4, half4, small_grads, grad_taps,
     ) = middle(length, attended, resid1, cotangent_here, small, kernel.shape[0], full_ud, full_sq)
-    layer_output = layer_output[None]
     input_grad, matrix_grads, square_grad, small_sums = back(
         heads, pos_heads, grad_out_head, prob, head_size, coarse, fine, small,
         signal, resid1, grad_res2, (normed1, hidden1, active1, normed2), (normed4, active4, grad_hidden4, half4),
         (out_time, grad_att_b, normed3, grad_pair, grad_conv_b, swish_b), small_grads, grad_taps, full_ud, full_sq,
     )
-    input_grad = input_grad[None]
-    upward_grad, downward_grad = matrix_grads[0], matrix_grads[1]
-    small_own = lax.dynamic_slice_in_dim(small_sums, place * share, share, 1)
-    vectors_grad = small_own[: vectors.shape[0]]
-    kernel_grad = small_own[vectors.shape[0] : vectors.shape[0] + kernel.shape[0]]
-    square_next, momentum_square, variance_square = adam_step(
-        square, square_grad, square_momentum, square_variance, DECAY_RATE
-    )
-    upward_next, momentum_upward, variance_upward = adam_step(
-        upward, upward_grad, upward_momentum, upward_variance, DECAY_RATE
-    )
-    downward_next, momentum_downward, variance_downward = adam_step(
-        downward, downward_grad, downward_momentum, downward_variance, DECAY_RATE
-    )
-    vectors_next, momentum_vectors, variance_vectors = adam_step(
-        vectors, vectors_grad, vectors_momentum, vectors_variance, 0.0
-    )
-    kernel_next, momentum_kernel, variance_kernel = adam_step(
-        kernel, kernel_grad, kernel_momentum, kernel_variance, DECAY_RATE
+    (
+        layer_output, input_grad,
+        square_grad, square_next, momentum_square, variance_square,
+        upward_grad, upward_next, momentum_upward, variance_upward,
+        downward_grad, downward_next, momentum_downward, variance_downward,
+        vectors_grad, vectors_next, momentum_vectors, variance_vectors,
+        kernel_grad, kernel_next, momentum_kernel, variance_kernel,
+    ) = finish(
+        layer_output, input_grad, matrix_grads, square_grad, small_sums,
+        (
+            (square, square_momentum, square_variance),
+            (upward, upward_momentum, upward_variance),
+            (downward, downward_momentum, downward_variance),
+            (vectors, vectors_momentum, vectors_variance),
+            (kernel.T, kernel_momentum.T, kernel_variance.T),
+        ),
     )
     return (
-        layer_output,
-        input_grad,
+        layer_output[None],
+        input_grad[None],
         square_grad,
         upward_grad,
         downward_grad,
         vectors_grad,
-        kernel_grad,
+        kernel_grad.T,
         square_next,
         upward_next,
         downward_next,
         vectors_next,
-        kernel_next,
+        kernel_next.T,
         momentum_square,
         variance_square,
         momentum_upward,
@@ -1433,8 +1507,8 @@
         variance_downward,
         momentum_vectors,
         variance_vectors,
-        momentum_kernel,
-        variance_kernel,
+        momentum_kernel.T,
+        variance_kernel.T,
     )
 
 

time: 263 us -> 245 us (0.932)
  local copies, waits for them, and re-layouts: 7.38 us -> 0 us
  other arithmetic: 8.15 us -> 2.26 us
  Pallas kernels: 245 us -> 241 us
    pallas_call x1, Pallas kernels: 95.5 us -> 89.6 us  [back(): pl.pallas_call(lambda *refs: back_kernel(head_size, *refs), name='back',...]
    unnamed x46 -> x0, local copies, waits for them, and re-layouts: 5.96 us -> none
    sub x3 -> x0, other arithmetic: 5.19 us -> none  [adam_step(): weight - LEARN_RATE * (update + decay * weight)]
    pallas_call x0 -> x1, Pallas kernels: none -> 4.32 us  [finish(): pl.pallas_call(lambda *refs: finish_kernel(states[3][0].shape[0], *refs),...]
    pallas_call x1, Pallas kernels: 96 us -> 92.6 us  [head(): pl.pallas_call(lambda *refs: head_kernel(head_size, *refs), name='head',...]
where the time goes in v1:
time: 245 us; the launch traced here: 244 us
  Pallas kernels  241 us (98%)
    pallas_call x1, Pallas kernels, head(): pl.pallas_call(lambda *refs: head_kernel(head_size, *refs), name='head',...  92.6 us
    pallas_call x1, Pallas kernels, back(): pl.pallas_call(lambda *refs: back_kernel(head_size, *refs), name='back',...  89.6 us
    pallas_call x1, Pallas kernels, middle(): pl.pallas_call(lambda *refs: middle_kernel(taps, *refs), name='middle', o...  54.1 us

profile of v1, /device:TPU:0, one launch (start us, length us, event | category | flops | bytes accessed | tf_op | source)
XLA Modules:
  0.0 244.4 jit_solution(7502765902306826805)
XLA Ops:
  1.3 0.3 fusion.1
  1.7 0.7 pad_maximum_fusion.1.refs_8_.refs_3_
  2.3 0.5 multiply_cosine_fusion
  2.9 0.7 pad_maximum_fusion.refs_9_.refs_4_
  3.6 92.6 %head.1 = (bf16[2,4096,512]{2,1,0:T(8,128)(2,1)}, bf16[16,2,128,512]{3,2,1,0:T(8,128)(2,1)}, f32[48,512]{1,0:T(8,128)}, bf16[256,512]{1,0:T(8,128)(2,1)}, bf16[2...) custom-call(f32[128,512]{1,0:T(8,128)} %refs_8_.1, ...), custom_call_target="tpu_custom_call" | custom-call | tf_op jit(solution)/shard_map/head/pallas_call | solution.py:1381
  96.2 54.1 %middle.1 = (bf16[256,512]{1,0:T(8,128)(2,1)}, f32[256,512]{1,0:T(8,128)}, bf16[1024,128]{1,0:T(8,128)(2,1)}, bf16[256,512]{1,0:T(8,128)(2,1)}, bf16[256,512]{1,...) custom-call(f32[8,128]{1,0:T(8,128)} %get-tuple-element.78.refs_0_, ...), custom_call_target="tpu_custom_call" | custom-call | tf_op jit(solution)/shard_map/middle/pallas_call | solution.py:484
  150.3 89.6 %back.1 = (f32[256,512]{1,0:T(8,128)}, f32[2,128,512]{2,1,0:T(8,128)}, f32[128,512]{1,0:T(8,128)}, f32[46,512]{1,0:T(8,128)}) custom-call(bf16[3,1024,128]{2,1,0:T(8,128)(2,1)} %get-tuple-element.86.refs_0_, bf16[2048,128]{1,0:T(8,128)(2,1)} %get-tuple-element.87.refs_1_, bf16[1024,128]{1,0:T(8,128)(2,1)} %get-tuple-element.88.refs_2_, ...), custom_call_target="tpu_custom_call" | custom-call | tf_op jit(solution)/shard_map/back/pallas_call | solution.py:946
  239.9 4.3 %finish.1 = (bf16[256,512]{1,0:T(8,128)(2,1)}, f32[256,512]{1,0:T(8,128)}, f32[128,512]{1,0:T(8,128)}, f32[128,512]{1,0:T(8,128)}, f32[128,512]{1,0:T(8,128)}, /...) custom-call(bf16[256,512]{1,0:T(8,128)(2,1)} %get-tuple-element.85.r, ...), custom_call_target="tpu_custom_call" | custom-call | tf_op jit(solution)/shard_map/finish/pallas_call | solution.py:1045
  (4 shorter events, 0.0 us)

commit v2 on v1

--- a/solution.py
+++ b/solution.py
@@ -1170,12 +1170,11 @@
             self.column(q, True, finish)
             self.along_a(q, finish)
         self.spread(self.high[0], finish, above)
-        self.column(self.high[0], False, finish, below)
+        self.column(self.high[0], True, finish, below)
         for q in self.low:
             self.along_b(q, finish)
         for q in self.high[1:]:
             self.column(q, False, finish, below)
-        self.spread(self.high[0], finish, below)
         for q in self.high[1:]:
             self.spread(q, finish)
 
@@ -1340,7 +1339,7 @@
         )
         keep(i).start()
         for k, q in enumerate(gather.high):
-            pl.when(i == min(2 * k + 1, nz - 1))(lambda: gather.along_b(q))
+            pl.when(i == min(k + 1, nz - 1))(lambda: gather.along_b(q))
         return 0
 
     lax.fori_loop(0, nz, attend, 0)

time: 245 us -> 241 us (0.984)
  Pallas kernels: 241 us -> 237 us
    pallas_call x1, Pallas kernels: 92.6 us -> 88.7 us  [head(): pl.pallas_call(lambda *refs: head_kernel(head_size, *refs), name='head',...]
where the time goes in v2:
time: 241 us
  Pallas kernels  237 us (98%)
    pallas_call x1, Pallas kernels, back(): pl.pallas_call(lambda *refs: back_kernel(head_size, *refs), name='back',...  89.1 us
    pallas_call x1, Pallas kernels, head(): pl.pallas_call(lambda *refs: head_kernel(head_size, *refs), name='head',...  88.7 us
    pallas_call x1, Pallas kernels, middle(): pl.pallas_call(lambda *refs: middle_kernel(taps, *refs), name='middle', o...  55.1 us

profile of v2, /device:TPU:0, one launch (start us, length us, event | category | flops | bytes accessed | tf_op | source)
XLA Modules:
  0.0 241.1 jit_solution(18011878541408756936)
XLA Ops:
  1.3 0.3 fusion.1
  1.7 0.7 pad_maximum_fusion.1.refs_8_.refs_3_
  2.3 0.5 multiply_cosine_fusion
  2.9 0.7 pad_maximum_fusion.refs_9_.refs_4_
  3.6 88.7 %head.1 = (bf16[2,4096,512]{2,1,0:T(8,128)(2,1)}, bf16[16,2,128,512]{3,2,1,0:T(8,128)(2,1)}, f32[48,512]{1,0:T(8,128)}, bf16[256,512]{1,0:T(8,128)(2,1)}, bf16[2...) custom-call(f32[128,512]{1,0:T(8,128)} %refs_8_.1, ...), custom_call_target="tpu_custom_call" | custom-call | tf_op jit(solution)/shard_map/head/pallas_call | solution.py:1380
  92.3 55.1 %middle.1 = (bf16[256,512]{1,0:T(8,128)(2,1)}, f32[256,512]{1,0:T(8,128)}, bf16[1024,128]{1,0:T(8,128)(2,1)}, bf16[256,512]{1,0:T(8,128)(2,1)}, bf16[256,512]{1,...) custom-call(f32[8,128]{1,0:T(8,128)} %get-tuple-element.78.refs_0_, ...), custom_call_target="tpu_custom_call" | custom-call | tf_op jit(solution)/shard_map/middle/pallas_call | solution.py:484
  147.4 89.1 %back.1 = (f32[256,512]{1,0:T(8,128)}, f32[2,128,512]{2,1,0:T(8,128)}, f32[128,512]{1,0:T(8,128)}, f32[46,512]{1,0:T(8,128)}) custom-call(bf16[3,1024,128]{2,1,0:T(8,128)(2,1)} %get-tuple-element.86.refs_0_, bf16[2048,128]{1,0:T(8,128)(2,1)} %get-tuple-element.87.refs_1_, bf16[1024,128]{1,0:T(8,128)(2,1)} %get-tuple-element.88.refs_2_, ...), custom_call_target="tpu_custom_call" | custom-call | tf_op jit(solution)/shard_map/back/pallas_call | solution.py:946
  236.6 4.3 %finish.1 = (bf16[256,512]{1,0:T(8,128)(2,1)}, f32[256,512]{1,0:T(8,128)}, f32[128,512]{1,0:T(8,128)}, f32[128,512]{1,0:T(8,128)}, f32[128,512]{1,0:T(8,128)}, /...) custom-call(bf16[256,512]{1,0:T(8,128)(2,1)} %get-tuple-element.85.r, ...), custom_call_target="tpu_custom_call" | custom-call | tf_op jit(solution)/shard_map/finish/pallas_call | solution.py:1045
  (4 shorter events, 0.0 us)

commit v3 on v2

--- a/solution.py
+++ b/solution.py
@@ -852,6 +852,7 @@
     matrix_terms(1, s1_ref, half1, 0, units)
     red.to_sibling(low, 1)
     red.along("a", high, 2)
+    red.along("a", low, 0)
     grad_add, gain0, shift0 = norm_backward(x_ref[...].astype(F32), gains, 0, grad_norm)
     away = jnp.logical_not(g.at_home())
     gx_buf[...] = (grad1 + grad_add).astype(BF)
@@ -868,7 +869,6 @@
     red.from_sibling(low, 1)
     red.along("b", low, 1)
     red.along("b", low, 2)
-    red.along("a", low, 0)
     meeting.start(1, meeting.total(0))
     red.along("z", high, 0)
     red.along("z", high, 1)
@@ -1339,7 +1339,7 @@
         )
         keep(i).start()
         for k, q in enumerate(gather.high):
-            pl.when(i == min(k + 1, nz - 1))(lambda: gather.along_b(q))
+            pl.when(i == min(k, nz - 1))(lambda: gather.along_b(q))
         return 0
 
     lax.fori_loop(0, nz, attend, 0)

time: 241 us -> 241 us (level)
  no operation moved by 1% of the time
where the time goes in v3:
time: 241 us
  Pallas kernels  237 us (98%)
    pallas_call x1, Pallas kernels, back(): pl.pallas_call(lambda *refs: back_kernel(head_size, *refs), name='back',...  89.1 us
    pallas_call x1, Pallas kernels, head(): pl.pallas_call(lambda *refs: head_kernel(head_size, *refs), name='head',...  88.7 us
    pallas_call x1, Pallas kernels, middle(): pl.pallas_call(lambda *refs: middle_kernel(taps, *refs), name='middle', o...  54.5 us

profile of v3, /device:TPU:0, one launch (start us, length us, event | category | flops | bytes accessed | tf_op | source)
XLA Modules:
  0.0 240.5 jit_solution(15314290780908725241)
XLA Ops:
  1.3 0.3 fusion.1
  1.7 0.7 pad_maximum_fusion.1.refs_8_.refs_3_
  2.3 0.5 multiply_cosine_fusion
  2.9 0.7 pad_maximum_fusion.refs_9_.refs_4_
  3.6 88.7 %head.1 = (bf16[2,4096,512]{2,1,0:T(8,128)(2,1)}, bf16[16,2,128,512]{3,2,1,0:T(8,128)(2,1)}, f32[48,512]{1,0:T(8,128)}, bf16[256,512]{1,0:T(8,128)(2,1)}, bf16[2...) custom-call(f32[128,512]{1,0:T(8,128)} %refs_8_.1, ...), custom_call_target="tpu_custom_call" | custom-call | tf_op jit(solution)/shard_map/head/pallas_call | solution.py:1380
  92.3 54.5 %middle.1 = (bf16[256,512]{1,0:T(8,128)(2,1)}, f32[256,512]{1,0:T(8,128)}, bf16[1024,128]{1,0:T(8,128)(2,1)}, bf16[256,512]{1,0:T(8,128)(2,1)}, bf16[256,512]{1,...) custom-call(f32[8,128]{1,0:T(8,128)} %get-tuple-element.78.refs_0_, ...), custom_call_target="tpu_custom_call" | custom-call | tf_op jit(solution)/shard_map/middle/pallas_call | solution.py:484
  146.9 89.1 %back.1 = (f32[256,512]{1,0:T(8,128)}, f32[2,128,512]{2,1,0:T(8,128)}, f32[128,512]{1,0:T(8,128)}, f32[46,512]{1,0:T(8,128)}) custom-call(bf16[3,1024,128]{2,1,0:T(8,128)(2,1)} %get-tuple-element.86.refs_0_, bf16[2048,128]{1,0:T(8,128)(2,1)} %get-tuple-element.87.refs_1_, bf16[1024,128]{1,0:T(8,128)(2,1)} %get-tuple-element.88.refs_2_, ...), custom_call_target="tpu_custom_call" | custom-call | tf_op jit(solution)/shard_map/back/pallas_call | solution.py:946
  236.0 4.3 %finish.1 = (bf16[256,512]{1,0:T(8,128)(2,1)}, f32[256,512]{1,0:T(8,128)}, f32[128,512]{1,0:T(8,128)}, f32[128,512]{1,0:T(8,128)}, f32[128,512]{1,0:T(8,128)}, /...) custom-call(bf16[256,512]{1,0:T(8,128)(2,1)} %get-tuple-element.85.r, ...), custom_call_target="tpu_custom_call" | custom-call | tf_op jit(solution)/shard_map/finish/pallas_call | solution.py:1045
  (4 shorter events, 0.0 us)
